TPU v7x, 32 devices: a whole 2x2x4 slice. The times are simulated.
32 devices in a mesh: mats: 8 (over z, x), tp: 4 (over y, core).
Axes of the slice: x: 2, y: 2, z: 4, core: 2. Of those that a mesh axis runs over, the one named last changes fastest.
Arguments:
- grad: bfloat16 [3072, 16384], P('tp', 'mats'), may hold values from -40 to 40
- momentum: float32 [3072, 16384], P('tp', 'mats'), may hold values from -6 to 6
Outputs:
- update: bfloat16 [3072, 16384], P('tp', 'mats')
- new_momentum: float32 [3072, 16384], P('tp', 'mats')
All inputs are finite; a program needn't handle non-finite values.
Results may differ from a plain program's by a relative error of at most 0.01.
Values may be sent and summed in bfloat16 or wider, within the bound.
A program may use at most 128 MiB of HBM per device.

v0:
```python
import functools
import math

import jax
import jax.numpy as jnp
from jax import lax
from jax.experimental import pallas as pl
from jax.experimental.pallas import tpu as pltpu
from jax.sharding import PartitionSpec as P

momentum_beta = 0.95
first_coef = 3.4445
second_coef = -4.775
third_coef = 2.0315
shape_gain = 0.2
epsilon = 1e-06


def row_dot(left, right):
    return lax.dot_general(
        left, right, (((1,), (1,)), ((), ())), preferred_element_type=jnp.float32
    )


def chain_kernel(tile, scale, bound_ref, gram_ref, x_ref, out_ref, base, held, left, right, saved):
    rows = x_ref.shape[0]
    bound = bound_ref[0, 0]
    root = lax.rsqrt(jnp.full((1, x_ref.shape[1]), bound, jnp.float32))
    inverse = root * root

    def tiles(body):
        @pl.loop(0, rows // tile)
        def _(step):
            body(pl.ds(pl.multiple_of(step * tile, tile), tile))

    def product(at, source):
        return inverse * jnp.dot(
            gram_ref[at, :], source[...], preferred_element_type=jnp.float32
        )

    def apply(source, target):
        def body(at):
            target[at, :] = product(at, source).astype(jnp.bfloat16)

        tiles(body)

    def combine(at, zeroth, once, twice):
        return (
            first_coef * zeroth[at, :].astype(jnp.float32)
            + second_coef * once[at, :].astype(jnp.float32)
            + third_coef * twice
        )

    def polynomial(source, target):
        apply(source, left)

        def body(at):
            target[at, :] = combine(at, source, left, product(at, left)).astype(jnp.bfloat16)

        tiles(body)

    def normalize(at):
        right[at, :] = (x_ref[at, :].astype(jnp.float32) * root).astype(jnp.bfloat16)

    tiles(normalize)
    polynomial(right, base)

    def start(at):
        held[at, :] = base[at, :]

    tiles(start)

    @pl.loop(0, 2)
    def _(turn):
        polynomial(held, right)
        polynomial(right, right)
        apply(right, held)

        @pl.when(turn == 0)
        def _():
            def keep(at):
                saved[at, :] = held[at, :]

            tiles(keep)

    def finish(at):
        mixed = combine(at, base, saved, held[at, :].astype(jnp.float32)).astype(jnp.bfloat16)
        out_ref[at, :] = (scale * mixed.astype(jnp.float32)).astype(jnp.bfloat16)

    tiles(finish)


def per_device(scale, grad, momentum):
    new_momentum = momentum_beta * momentum + grad.astype(jnp.float32)
    iterate = (grad.astype(jnp.float32) + momentum_beta * new_momentum).astype(jnp.bfloat16)
    columns = lax.all_gather(iterate, "tp", axis=0, tiled=True)
    part = row_dot(iterate, columns).astype(jnp.bfloat16)
    share = lax.psum_scatter(part, "mats", scatter_dimension=0, tiled=True)
    peak = jnp.max(jnp.sum(jnp.abs(share.astype(jnp.float32)), axis=1))
    bound = lax.pmax(peak, ("tp", "mats")) + epsilon
    gram = lax.all_gather(share, ("tp", "mats"), axis=0, tiled=True)
    rows = columns.shape[0]
    width = columns.shape[1] // lax.axis_size("tp")
    own = lax.dynamic_slice_in_dim(columns, lax.axis_index("tp") * width, width, axis=1)
    tile = math.gcd(rows, 512)
    whole = pl.BlockSpec(memory_space=pltpu.VMEM)
    result = pl.pallas_call(
        functools.partial(chain_kernel, tile, scale),
        out_shape=jax.ShapeDtypeStruct(own.shape, jnp.bfloat16),
        in_specs=[pl.BlockSpec(memory_space=pltpu.SMEM), whole, whole],
        out_specs=whole,
        scratch_shapes=[pltpu.VMEM(own.shape, jnp.bfloat16)] * 5,
        compiler_params=pltpu.CompilerParams(vmem_limit_bytes=60 * 1024 * 1024),
        cost_estimate=pl.CostEstimate(
            flops=24 * rows * rows * width, bytes_accessed=2 * rows * rows, transcendentals=0
        ),
    )(bound.reshape(1, 1), gram, own)
    update = lax.all_to_all(result, "tp", 0, 1, tiled=True)
    return (update, new_momentum)


def solution(mesh):
    def step(grad, momentum):
        scale = shape_gain * math.sqrt(max(grad.shape))
        return jax.shard_map(
            functools.partial(per_device, scale),
            mesh=mesh,
            in_specs=(P("tp", "mats"), P("tp", "mats")),
            out_specs=(P("tp", "mats"), P("tp", "mats")),
            check_vma=False,
        )(grad, momentum)

    return step
```

profile of v0, /device:TPU:0, one launch (start us, length us, event | category | flops | bytes accessed | tf_op | source)
XLA Modules:
  0.0 533.4 jit_solution(10666718813383570961)
XLA Ops:
  7.2 0.0 all-gather.3.cloned.1.call-start
  7.2 9.3 %fusion = (bf16[768,2048]{1,0:T(8,128)(2,1)}, f32[768,2048]{1,0:T(8,128)}) fusion(bf16[768,2048]{1,0:T(8,128)(2,1)} %param.2, f32[768,2048]{1,0:T(8,128)} %param.3), kind=kLoop, calls=%fused_computation.2 | loop fusion | flops 9437184 | bytes 18874368 | tf_op jit(solution)/shard_map/convert_element_type | solution.py:95
  16.5 0.0 all-gather.3.cloned.1.call-update
  16.5 0.0 reduce-scatter.2.cloned.1.call-start
  16.5 84.9 %all-gather.3.cloned.1.call-done = bf16[3072,2048]{1,0:T(8,128)(2,1)} async-done(((bf16[768,2048]{1,0:T(8,128)(2,1)}), bf16[3072,2048]{1,0:T(8,128)(2,1)}) %all-gather.3.cloned.1.call-update) | async-done | bytes 12582928 | tf_op jit(solution)/shard_map/all_gather | solution.py:96
  101.5 15.3 %convolution_convert_fusion = bf16[768,3072]{1,0:T(8,128)(2,1)} fusion(bf16[768,2048]{1,0:T(8,128)(2,1)} %get-tuple-element.2, bf16[3072,2048]{1,0:T(8,128)(2,1)} %all-gather.3.cloned.1.call-done), kind=kOutput, calls=%fused_computation.3 | convolution fusion | flops 9666035712 | bytes 20447232 | tf_op jit(solution)/shard_map/dot_general | solution.py:20
  116.8 0.0 reduce-scatter.2.cloned.1.call-update
  116.8 0.0 all-gather.5.cloned.1.call-start
  116.8 96.2 %reduce-scatter.2.cloned.1.call-done = bf16[96,3072]{1,0:T(8,128)(2,1)} async-done(((bf16[768,3072]{1,0:T(8,128)(2,1)}), bf16[96,3072]{1,0:T(8,128)(2,1)}) %reduce-scatter.2.cloned.1.call-update) | async-done | bytes 589840 | tf_op jit(solution)/shard_map/reduce_scatter | solution.py:98
  213.0 0.0 all-gather.5.cloned.1.call-update
  213.0 1.3 abs_reduce_fusion
  214.3 0.7 reduce_max.9
  215.0 3.8 constant_dynamic-slice_fusion.x_ref
  218.7 42.3 %pmax.7 = f32[]{:T(128)} all-reduce(f32[]{:T(128)} %reduce_max.9), channel_id=1, replica_groups=mesh['mats'=8,'tp'=4] {'tp','mats'}, use_global_device_ids=true, to_apply=%region_3.0 | all-reduce | flops 1 | bytes 8 | tf_op jit(solution)/shard_map/pmax | solution.py:100
  261.7 78.8 %all-gather.5.cloned.1.call-done.gram_ref = bf16[3072,3072]{1,0:T(8,128)(2,1)} async-done(((bf16[96,3072]{1,0:T(8,128)(2,1)}), bf16[3072,3072]{1,0:T(8,128)(2,1)}) %all-gather.5.cloned.1.call-update) | async-done | bytes 18874384 | tf_op jit(solution)/shard_map/all_gather | solution.py:101
  340.5 143.6 %shard_map.41 = bf16[3072,512]{1,0:T(8,128)(2,1)} custom-call(f32[1,1]{1,0:T(1,128)} %bitcast.bound_ref, bf16[3072,3072]{1,0:T(8,128)(2,1)} %all-gather.5.cloned.1.call-done.gram_ref, bf16[3072,512]{1,0:T(8,128)(2,1)} %constant_dynamic-slice_fusion.x_ref), custom_call_target="tpu_custom_call" | custom-call | flops 115964116992 | bytes 18874368 | tf_op jit(solution)/shard_map/pallas_call | solution.py:107
  484.2 40.6 %all_to_all.19 = bf16[4,768,512]{2,1,0:T(8,128)(2,1)S(1)} all-to-all(bf16[4,768,512]{2,1,0:T(8,128)(2,1)} %bitcast.9), channel_id=1, replica_groups=mesh['mats'=8,'tp'=4] {'tp'}, dimensions={0} | all-to-all | bytes 6291456 | tf_op jit(solution)/shard_map/all_to_all | solution.py:118
  524.7 2.1 copy.5
Async XLA Ops:
  7.2 94.3 %all-gather.3.cloned.1.call-start = ((), (), s32[]{:S(2)}) async-start(), calls=%async_computation.2 | async-start | bytes 15728640 | tf_op jit(solution)/shard_map/all_gather | solution.py:96
  16.5 196.5 %reduce-scatter.2.cloned.1.call-start = ((), (), s32[]{:S(2)}) async-start(), calls=%async_computation.3 | async-start | bytes 5308416 | tf_op jit(solution)/shard_map/reduce_scatter | solution.py:98
  116.8 223.7 %all-gather.5.cloned.1.call-start = ((), (), s32[]{:S(2)}) async-start(), calls=%async_computation.4 | async-start | bytes 19464192 | tf_op jit(solution)/shard_map/all_gather | solution.py:101
Sparse Core Ops, SparseCore 0:
  16.6 84.7 all-gather.2
  116.9 96.0 reduce-scatter.1
  216.0 124.4 all-gather.4
where the time goes:
time: 534 us; the launch traced here: 533 us
  waiting for transfers between devices  260 us (49%)
  Pallas kernels  144 us (27%)
  blocking collectives  82.8 us (16%)
  matrix products  15.3 us (3%)
  between operations  14.4 us (3%)
  other arithmetic  11.2 us (2%)
  local copies, waits for them, and re-layouts  5.9 us (1%)
    pallas_call x1, Pallas kernels, per_device(): pl.pallas_call(functools.partial(chain_kernel, tile, scale), out_shape=ja...  144 us
    reduce_scatter x1, waiting for transfers between devices, per_device(): share = lax.psum_scatter(part, 'mats', scatter_dimension=0, tiled=True)  96.2 us
    all_gather x1, waiting for transfers between devices, per_device(): columns = lax.all_gather(iterate, 'tp', axis=0, tiled=True)  84.9 us
    all_gather x1, waiting for transfers between devices, per_device(): gram = lax.all_gather(share, ('tp', 'mats'), axis=0, tiled=True)  78.8 us
    pmax x1, blocking collectives, per_device(): bound = lax.pmax(peak, ('tp', 'mats')) + epsilon  42.3 us
    all_to_all x1, blocking collectives, per_device(): update = lax.all_to_all(result, 'tp', 0, 1, tiled=True)  40.6 us
    dot_general x1, matrix products, row_dot(): lax.dot_general(left, right, (((1,), (1,)), ((), ())), preferred_element_...  15.3 us
  transfers between devices with their start and end apart: 3, of which 3 were waited for; matrix products, arithmetic and copies ran while one was open for 1% of the time, Pallas kernels for 0%

commit v1 on v0

v1 whole, which is shorter than its diff:
```python
import functools
import math

import jax
import jax.numpy as jnp
from jax import lax
from jax.experimental import pallas as pl
from jax.experimental.pallas import tpu as pltpu
from jax.sharding import PartitionSpec as P

momentum_beta = 0.95
first_coef = 3.4445
second_coef = -4.775
third_coef = 2.0315
shape_gain = 0.2
epsilon = 1e-06
grant = 62 * 1024 * 1024


def nt_dot(left, right):
    return lax.dot_general(
        left, right, (((1,), (1,)), ((), ())), preferred_element_type=jnp.float32
    )


def window_of(blocks):
    return blocks // 2 + 1


def gram_kernel(block, where_ref, x_ref, part_ref):
    blocks = x_ref.shape[0] // block
    mine = part_ref.shape[0] // block
    window = part_ref.shape[1] // block
    first = where_ref[0] * mine
    left_at = pl.ds(pl.multiple_of(first * block, block), mine * block)
    for j in range(mine + window - 1):
        low, high = max(0, j - window + 1), min(mine - 1, j)
        other = lax.rem(first + j, blocks)
        right = x_ref[pl.ds(pl.multiple_of(other * block, block), block), :]
        rows = pl.ds(
            pl.multiple_of((first + low) * block, block), (high - low + 1) * block
        )
        product = nt_dot(x_ref[rows, :], right).astype(jnp.bfloat16)
        for i in range(low, high + 1):
            at = (i - low) * block
            part_ref[i * block : (i + 1) * block, (j - i) * block : (j - i + 1) * block] = (
                product[at : at + block, :]
            )


def poly_kernel(block, scale, where_ref, compact_ref, out_ref, kappa_ref, gram, own, one, two, left, right):
    size = gram.shape[0]
    blocks = size // block
    window = compact_ref.shape[1] // block
    for i in range(blocks):
        for d in range(window):
            j = (i + d) % blocks
            tile = compact_ref[i * block : (i + 1) * block, d * block : (d + 1) * block]
            gram[i * block : (i + 1) * block, j * block : (j + 1) * block] = tile
            if d > 0 and 2 * d != blocks:
                gram[j * block : (j + 1) * block, i * block : (i + 1) * block] = tile.T

    def column_sums(step, total):
        rows = jnp.abs(gram[pl.ds(pl.multiple_of(step * 16, 16), 16), :].astype(jnp.float32))
        return total + (rows[0:8] + rows[8:16])

    total = lax.fori_loop(0, size // 16, column_sums, jnp.zeros((8, size), jnp.float32))
    bound = jnp.max(jnp.sum(total, axis=0, keepdims=True), axis=1, keepdims=True) + epsilon
    root = lax.rsqrt(jnp.broadcast_to(bound, (1, 128)))
    kappa = (scale * first_coef * first_coef) * root
    kappa_ref[...] = kappa
    inverse = (root * root)[:, :1]
    count = own.shape[0]
    width = math.gcd(size, 1024)

    def columns(body):
        @pl.loop(0, size // width)
        def _(step):
            body(pl.ds(pl.multiple_of(step * width, width), width))

    def times_gram(source, at):
        return inverse * jnp.dot(source[...], gram[:, at], preferred_element_type=jnp.float32)

    def wide(ref, at):
        return ref[:, at].astype(jnp.float32)

    def apply(source, target, constant=None):
        def body(at):
            value = times_gram(source, at)
            if constant is not None:
                value = value + (constant * inverse) * wide(own, at)
            target[:, at] = value.astype(jnp.bfloat16)

        columns(body)

    def polynomial(source, middle, target):
        apply(source, middle)

        def body(at):
            target[:, at] = (
                first_coef * wide(source, at)
                + second_coef * wide(middle, at)
                + third_coef * times_gram(middle, at)
            ).astype(jnp.bfloat16)

        columns(body)

    if count % 16 == 0:
        own[...] = gram[pl.ds(pl.multiple_of(where_ref[0] * count, 16), count), :]
    else:
        row = lax.broadcasted_iota(jnp.int32, (count, size), 0) + where_ref[0] * count
        column = lax.broadcasted_iota(jnp.int32, (count, size), 1)
        two[...] = (row == column).astype(jnp.float32).astype(jnp.bfloat16)

        def select(at):
            own[:, at] = jnp.dot(
                two[...], gram[:, at], preferred_element_type=jnp.float32
            ).astype(jnp.bfloat16)

        columns(select)

    def start(at):
        left[:, at] = (inverse * wide(own, at)).astype(jnp.bfloat16)

    columns(start)

    def first(at):
        one[:, at] = (
            second_coef * wide(left, at) + third_coef * times_gram(left, at)
        ).astype(jnp.bfloat16)

    columns(first)
    apply(one, left, first_coef)
    polynomial(left, right, two)
    polynomial(two, right, left)

    def keep(at):
        two[:, at] = left[:, at]

    columns(keep)
    apply(two, right)
    polynomial(right, left, own)
    polynomial(own, left, right)

    def finish(at):
        mixed = (
            first_coef * wide(one, at) + second_coef * wide(two, at) + third_coef * wide(right, at)
        )
        out_ref[:, at] = ((scale * root[:, :1]) * mixed).astype(jnp.bfloat16)

    columns(finish)


def per_device(scale, grad, momentum):
    new_momentum = momentum_beta * momentum + grad.astype(jnp.float32)
    iterate = (grad.astype(jnp.float32) + momentum_beta * new_momentum).astype(jnp.bfloat16)
    columns = lax.all_gather(iterate, "tp", axis=0, tiled=True)
    size = columns.shape[0]
    mine = iterate.shape[0]
    block = math.gcd(mine, 256)
    window = window_of(size // block) * block
    smem = pl.BlockSpec(memory_space=pltpu.SMEM)
    whole = pl.BlockSpec(memory_space=pltpu.VMEM)
    params = pltpu.CompilerParams(vmem_limit_bytes=grant)
    tp = lax.axis_index("tp")
    part = pl.pallas_call(
        functools.partial(gram_kernel, block),
        out_shape=jax.ShapeDtypeStruct((mine, window), jnp.bfloat16),
        in_specs=[smem, whole],
        out_specs=whole,
        compiler_params=params,
        name="gram",
    )(tp.reshape(1), columns)
    share = lax.psum_scatter(part, "mats", scatter_dimension=0, tiled=True)
    compact = lax.all_gather(share, ("tp", "mats"), axis=0, tiled=True)
    count = share.shape[0]
    place = tp * lax.axis_size("mats") + lax.axis_index("mats")
    thin = pltpu.VMEM((count, size), jnp.bfloat16)
    rows, kappa = pl.pallas_call(
        functools.partial(poly_kernel, block, scale),
        out_shape=(
            jax.ShapeDtypeStruct((count, size), jnp.bfloat16),
            jax.ShapeDtypeStruct((1, 128), jnp.float32),
        ),
        in_specs=[smem, whole],
        out_specs=(whole, whole),
        scratch_shapes=[pltpu.VMEM((size, size), jnp.bfloat16)] + [thin] * 5,
        compiler_params=params,
        cost_estimate=pl.CostEstimate(
            flops=22 * count * size * size, bytes_accessed=size * window * 2, transcendentals=0
        ),
        name="poly",
    )(place.reshape(1), compact)
    matrix = lax.all_gather(rows, "mats", axis=0, tiled=True)
    product = jnp.dot(matrix, columns, preferred_element_type=jnp.float32)
    update = (product + kappa[0, 0] * iterate.astype(jnp.float32)).astype(jnp.bfloat16)
    return (update, new_momentum)


def solution(mesh):
    def step(grad, momentum):
        scale = shape_gain * math.sqrt(max(grad.shape))
        return jax.shard_map(
            functools.partial(per_device, scale),
            mesh=mesh,
            in_specs=(P("tp", "mats"), P("tp", "mats")),
            out_specs=(P("tp", "mats"), P("tp", "mats")),
            check_vma=False,
        )(grad, momentum)

    return step
```

time: 534 us -> 429 us (0.80)
  blocking collectives: 82.8 us -> 0 us
  Pallas kernels: 144 us -> 63.4 us
  waiting for transfers between devices: 260 us -> 325 us
  local copies, waits for them, and re-layouts: 5.9 us -> 0 us
    all_gather x1 -> x2, waiting for transfers between devices: 78.8 us -> 168 us  [the longest x1 90.1 us: per_device(): compact = lax.all_gather(share, ('tp', 'mats'), axis=0, tiled=True)]
    pallas_call x1 -> x2, Pallas kernels: 144 us -> 63.4 us  [the longest x1 51.5 us: per_device(): pl.pallas_call(functools.partial(poly_kernel, block, scale), out_shape=(j...]
    pmax x1 -> x0, blocking collectives: 42.3 us -> none  [per_device(): bound = lax.pmax(peak, ('tp', 'mats')) + epsilon]
    all_to_all x1 -> x0, blocking collectives: 40.6 us -> none  [per_device(): update = lax.all_to_all(result, 'tp', 0, 1, tiled=True)]
    reduce_scatter x1, waiting for transfers between devices: 96.2 us -> 71.9 us  [per_device(): share = lax.psum_scatter(part, 'mats', scatter_dimension=0, tiled=True)]
  transfers between devices with their start and end apart: 3 -> 4, of which waited for: 3 -> 4; matrix products, arithmetic and copies ran while one was open for 1% -> 0% of each run, Pallas kernels for 0% -> 0%
where the time goes in v1:
time: 429 us
  waiting for transfers between devices  325 us (76%)
  Pallas kernels  63.4 us (15%)
  matrix products  16.7 us (4%)
  between operations  13.8 us (3%)
  other arithmetic  9.26 us (2%)
    all_gather x1, waiting for transfers between devices, per_device(): compact = lax.all_gather(share, ('tp', 'mats'), axis=0, tiled=True)  90.1 us
    all_gather x1, waiting for transfers between devices, per_device(): columns = lax.all_gather(iterate, 'tp', axis=0, tiled=True)  84.9 us
    all_gather x1, waiting for transfers between devices, per_device(): matrix = lax.all_gather(rows, 'mats', axis=0, tiled=True)  78.1 us
    reduce_scatter x1, waiting for transfers between devices, per_device(): share = lax.psum_scatter(part, 'mats', scatter_dimension=0, tiled=True)  71.9 us
    pallas_call x1, Pallas kernels, per_device(): pl.pallas_call(functools.partial(poly_kernel, block, scale), out_shape=(j...  51.5 us
    dot_general x1, matrix products, per_device(): product = jnp.dot(matrix, columns, preferred_element_type=jnp.float32)  16.7 us
    pallas_call x1, Pallas kernels, per_device(): pl.pallas_call(functools.partial(gram_kernel, block), out_shape=jax.Shape...  12 us
    convert_element_type x1, other arithmetic, per_device(): (grad.astype(jnp.float32) + momentum_beta * new_momentum).astype(jnp.bflo...  9.26 us
  transfers between devices with their start and end apart: 4, of which 4 were waited for; matrix products, arithmetic and copies ran while one was open for 0% of the time, Pallas kernels for 0%

profile of v1, /device:TPU:0, one launch (start us, length us, event | category | flops | bytes accessed | tf_op | source)
XLA Modules:
  0.0 428.6 jit_solution(3233935004684373690)
XLA Ops:
  7.2 0.0 all-gather.4.cloned.1.call-start
  7.2 9.3 %fusion = (bf16[768,2048]{1,0:T(8,128)(2,1)}, f32[768,2048]{1,0:T(8,128)}) fusion(bf16[768,2048]{1,0:T(8,128)(2,1)} %param.2, f32[768,2048]{1,0:T(8,128)} %param.3), kind=kLoop, calls=%fused_computation.2 | loop fusion | flops 9437184 | bytes 18874368 | tf_op jit(solution)/shard_map/convert_element_type | solution.py:156
  16.5 0.0 all-gather.4.cloned.1.call-update
  16.5 0.0 reduce-scatter.2.cloned.1.call-start
  16.5 84.9 %all-gather.4.cloned.1.call-done.x_ref = bf16[3072,2048]{1,0:T(8,128)(2,1)} async-done(((bf16[768,2048]{1,0:T(8,128)(2,1)}), bf16[3072,2048]{1,0:T(8,128)(2,1)}) %all-gather.4.cloned.1.call-update) | async-done | bytes 12582928 | tf_op jit(solution)/shard_map/all_gather | solution.py:157
  101.5 12.0 %gram.1 = bf16[768,1792]{1,0:T(8,128)(2,1)} custom-call(s32[1]{0:T(128)} %bitcast.1.where_ref, bf16[3072,2048]{1,0:T(8,128)(2,1)} %all-gather.4.cloned.1.call-done.x_ref), custom_call_target="tpu_custom_call" | custom-call | tf_op jit(solution)/shard_map/gram/pallas_call | solution.py:166
  113.4 0.0 reduce-scatter.2.cloned.1.call-update
  113.5 0.0 all-gather.6.cloned.1.call-start
  113.5 71.9 %reduce-scatter.2.cloned.1.call-done = bf16[96,1792]{1,0:T(8,128)(2,1)} async-done(((bf16[768,1792]{1,0:T(8,128)(2,1)}), bf16[96,1792]{1,0:T(8,128)(2,1)}) %reduce-scatter.2.cloned.1.call-update) | async-done | bytes 344080 | tf_op jit(solution)/shard_map/reduce_scatter | solution.py:174
  185.5 0.0 all-gather.6.cloned.1.call-update
  185.5 0.2 all-gather.8.cloned.1.call-start
  185.7 90.1 %all-gather.6.cloned.1.call-done.compact_ref = bf16[3072,1792]{1,0:T(8,128)(2,1)} async-done(((bf16[96,1792]{1,0:T(8,128)(2,1)}), bf16[3072,1792]{1,0:T(8,128)(2,1)}) %all-gather.6.cloned.1.call-update) | async-done | bytes 11010064 | tf_op jit(solution)/shard_map/all_gather | solution.py:175
  275.9 51.5 %poly.1 = (bf16[96,3072]{1,0:T(8,128)(2,1)}, f32[1,128]{1,0:T(1,128)}) custom-call(s32[1]{0:T(128)} %bitcast.where_ref, bf16[3072,1792]{1,0:T(8,128)(2,1)} %all-gather.6.cloned.1.call-done.compact_ref), custom_call_target="tpu_custom_call" | custom-call | flops 19931332608 | bytes 11010048 | tf_op jit(solution)/shard_map/poly/pallas_call | solution.py:179
  327.3 0.0 all-gather.8.cloned.1.call-update
  327.3 78.1 %all-gather.8.cloned.1.call-done = bf16[768,3072]{1,0:T(8,128)(2,1)} async-done(((bf16[96,3072]{1,0:T(8,128)(2,1)}), bf16[768,3072]{1,0:T(8,128)(2,1)}) %all-gather.8.cloned.1.call-update) | async-done | bytes 4718608 | tf_op jit(solution)/shard_map/all_gather | solution.py:194
  405.4 16.7 %add_convert_fusion = bf16[768,2048]{1,0:T(8,128)(2,1)} fusion(bf16[768,2048]{1,0:T(8,128)(2,1)} %get-tuple-element.6, bf16[768,3072]{1,0:T(8,128)(2,1)} %all-gather.8.cloned.1.call-done, bf16[3072,2048]{1,0:T(8,128)(2,1)} %all-gather.4.cloned.1.call-done.x_ref, f32[]{:T(128)} %bitcast.6), kind=kOutput, calls=%fused_computation.3 | convolution fusion | flops 9669967872 | bytes 23592964 | tf_op jit(solution)/shard_map/dot_general | solution.py:195
Async XLA Ops:
  7.2 94.3 %all-gather.4.cloned.1.call-start = ((), (), s32[]{:S(2)}) async-start(), calls=%async_computation.1 | async-start | bytes 15728640 | tf_op jit(solution)/shard_map/all_gather | solution.py:157
  16.5 169.0 %reduce-scatter.2.cloned.1.call-start = ((), (), s32[]{:S(2)}) async-start(), calls=%async_computation.2 | async-start | bytes 3096576 | tf_op jit(solution)/shard_map/reduce_scatter | solution.py:174
  113.5 162.4 %all-gather.6.cloned.1.call-start = ((), (), s32[]{:S(2)}) async-start(), calls=%async_computation.3 | async-start | bytes 11354112 | tf_op jit(solution)/shard_map/all_gather | solution.py:175
  185.5 219.9 %all-gather.8.cloned.1.call-start = ((), (), s32[]{:S(2)}) async-start(), calls=%async_computation.4 | async-start | bytes 5308416 | tf_op jit(solution)/shard_map/all_gather | solution.py:194
Sparse Core Ops, SparseCore 0:
  16.6 84.7 all-gather.3
  113.6 71.8 reduce-scatter.1
  188.4 87.3 all-gather.5
  327.4 77.8 all-gather.7

commit v2 on v1

--- a/solution.py
+++ b/solution.py
@@ -15,6 +15,218 @@
 shape_gain = 0.2
 epsilon = 1e-06
 grant = 62 * 1024 * 1024
+
+
+def digits_of(mesh):
+    table = {}
+    shape = mesh.devices.shape
+    for number, axis in enumerate(mesh.axis_names):
+        extent = shape[number]
+        line = [mesh.devices[tuple(i if k == number else 0 for k in range(len(shape)))] for i in range(extent)]
+        found = []
+        if all(hasattr(device, "coords") for device in line):
+            places = [(*device.coords, device.core_on_chip) for device in line]
+            for place, column in enumerate(zip(*places)):
+                kinds = len(set(column))
+                if kinds > 1:
+                    stride = next(i for i in range(extent) if column[i] != column[0])
+                    if all((i // stride) % kinds == column[i] - column[0] for i in range(extent)):
+                        found.append((axis, stride, kinds, place == 3))
+        if math.prod(kinds for _, _, kinds, _ in found) != extent:
+            found = [(axis, 1, extent, False)]
+        table[axis] = sorted(found, key=lambda digit: -digit[1])
+    return table
+
+
+def place(digit):
+    axis, stride, extent, _ = digit
+    return lax.rem(lax.div(lax.axis_index(axis), stride), extent)
+
+
+def moves(digit):
+    here, extent = place(digit), digit[2]
+    if extent == 2:
+        return [(1 - 2 * here, None)]
+    return [(1, here + 1 < extent), (-1, here >= 1)]
+
+
+def when(condition, body):
+    if condition is None:
+        body()
+    else:
+        pl.when(condition)(body)
+
+
+def both(*conditions):
+    found = [c for c in conditions if c is not None]
+    return functools.reduce(lambda a, b: a & b, found) if found else None
+
+
+def peer(digit, offset):
+    axis, stride, _, _ = digit
+    return {axis: lax.axis_index(axis) + offset * stride}
+
+
+def barrier_all(digits):
+    semaphore = pltpu.get_barrier_semaphore()
+    for digit in digits:
+        for offset, has in moves(digit):
+            when(has, functools.partial(
+                pl.semaphore_signal, semaphore, inc=1, device_id=peer(digit, offset),
+                device_id_type=pl.DeviceIdType.MESH))
+    count = 0
+    for digit in digits:
+        for _, has in moves(digit):
+            count = count + (1 if has is None else has.astype(jnp.int32))
+    pl.semaphore_wait(semaphore, count)
+
+
+def relatives(digit):
+    here, extent = place(digit), digit[2]
+    if extent == 2:
+        return [(1, 2 * here - 1, 1 - here, None)]
+    found = []
+    for hop in range(1, extent):
+        found.append((hop, 1, here - hop, here >= hop))
+        found.append((hop, -1, here + hop, here + hop < extent))
+    return found
+
+
+class Gather:
+    def __init__(self, layout, pieces, buffer, source, send_sem, recv_sem):
+        self.layout, self.pieces, self.buffer, self.source = layout, pieces, buffer, source
+        self.send_sem, self.recv_sem = send_sem, recv_sem
+        self.sent = []
+
+    @staticmethod
+    def semaphores(layout, pieces):
+        dims = tuple(d[2] for d in layout)
+        return [
+            pltpu.SemaphoreType.DMA((len(pieces), 2 * len(layout)) + dims),
+            pltpu.SemaphoreType.DMA((len(pieces),) + dims),
+        ]
+
+    def copy(self, piece, block, digit, offset, way, own):
+        order, row, count = self.pieces[piece]
+        index = tuple(block[d] for d in self.layout)
+        rows = (pl.ds(row, count), slice(None))
+        at = self.buffer.at[index + rows]
+        lane = 2 * self.layout.index(digit) + way
+        return pltpu.make_async_remote_copy(
+            src_ref=self.source.at[rows] if own else at,
+            dst_ref=at,
+            send_sem=self.send_sem.at[(piece, lane) + index],
+            recv_sem=self.recv_sem.at[(piece,) + index],
+            device_id=peer(digit, offset),
+            device_id_type=pl.DeviceIdType.MESH,
+        )
+
+    def send(self, piece, block, exists, digit, directions, own=False):
+        for way, (offset, has) in enumerate(moves(digit)):
+            if directions is not None and way not in directions:
+                continue
+            copy = self.copy(piece, block, digit, offset, way, own)
+            condition = both(exists, has)
+            when(condition, copy.start)
+            self.sent.append((condition, copy))
+
+    def events(self, piece):
+        order = self.pieces[piece][0]
+        here = {d: place(d) for d in order}
+        found = []
+
+        def begin(after):
+            for digit in order:
+                self.send(piece, here, None, digit, None, own=True)
+
+        found.append((0, begin))
+
+        def arrivals(stage, block, exists, depth):
+            digit = order[stage]
+            for hop, travel, q, there in relatives(digit):
+                source = {**block, digit: q}
+                condition = both(exists, there)
+
+                def arrive(after, stage=stage, digit=digit, source=source, condition=condition, hop=hop, travel=travel):
+                    offset, _ = moves(digit)[0]
+                    when(condition, self.copy(piece, source, digit, offset, 0, False).wait_recv)
+                    if digit[2] > 2:
+                        self.send(piece, source, condition, digit, (0 if travel > 0 else 1,))
+                    for later in order[stage + 1 :]:
+                        self.send(piece, source, condition, later, None)
+                    if after is not None:
+                        after(piece, source, condition)
+
+                found.append((depth + hop, arrive))
+
+        def expand(stage, earlier, block, exists, depth):
+            if earlier == stage:
+                arrivals(stage, block, exists, depth)
+                return
+            digit = order[earlier]
+            expand(stage, earlier + 1, {**block, digit: here[digit]}, exists, depth)
+            for hop, _, q, there in relatives(digit):
+                expand(stage, earlier + 1, {**block, digit: q}, both(exists, there), depth + hop)
+
+        for stage in range(len(order)):
+            expand(stage, 0, dict(here), None, 0)
+        return found
+
+    def run(self, after=None):
+        queue = []
+        for piece in range(len(self.pieces)):
+            for depth, action in self.events(piece):
+                queue.append((depth, piece, len(queue), action))
+        for _, _, _, action in sorted(queue, key=lambda entry: entry[:3]):
+            action(after)
+
+    def drain(self):
+        for condition, copy in self.sent:
+            when(condition, copy.wait_send)
+
+
+def gather_kernel(layout, pieces, x_ref, out_ref, send_sem, recv_sem, local_sem):
+    barrier_all(layout)
+    gather = Gather(layout, pieces, out_ref, x_ref, send_sem, recv_sem)
+    gather.run()
+    local = pltpu.make_async_copy(x_ref, out_ref.at[tuple(place(d) for d in layout)], local_sem)
+    local.start()
+    local.wait()
+    gather.drain()
+
+
+def pieces_of(rows, orders, chunks):
+    units = max(1, rows // 16)
+    chunks = min(chunks, units)
+    cuts = [units * i // chunks * 16 for i in range(chunks)] + [rows]
+    return [(orders[i % len(orders)], cuts[i], cuts[i + 1] - cuts[i]) for i in range(chunks)]
+
+
+def events_of(order):
+    total, held = 0, 1
+    for digit in order:
+        around = 1 if digit[2] == 2 else 2 * (digit[2] - 1)
+        total += held * around
+        held *= 1 + around
+    return total
+
+
+def gather(x, axes, layout, orders, chunks, ident, name):
+    rows, columns = x.shape
+    if rows % 16 or len(orders) * events_of(orders[0]) > 256:
+        return lax.all_gather(x, axes, axis=0, tiled=True)
+    pieces = pieces_of(rows, orders, chunks)
+    dims = tuple(d[2] for d in layout)
+    out = pl.pallas_call(
+        functools.partial(gather_kernel, layout, pieces),
+        out_shape=jax.ShapeDtypeStruct(dims + (rows, columns), x.dtype),
+        in_specs=[pl.BlockSpec(memory_space=pltpu.VMEM)],
+        out_specs=pl.BlockSpec(memory_space=pl.ANY),
+        scratch_shapes=Gather.semaphores(layout, pieces) + [pltpu.SemaphoreType.DMA],
+        compiler_params=pltpu.CompilerParams(collective_id=ident, has_side_effects=True),
+        name=name,
+    )(x)
+    return out.reshape(math.prod(dims) * rows, columns)
 
 
 def nt_dot(left, right):
@@ -151,10 +363,21 @@
     columns(finish)
 
 
-def per_device(scale, grad, momentum):
+def orders_of(digits):
+    layout = tuple(digits["tp"]) + tuple(digits["mats"])
+    far = {axis: [d for d in found if not d[3]] for axis, found in digits.items()}
+    near = [d for d in layout if d[3]]
+    one = tuple(far["mats"] + far["tp"] + near)
+    two = tuple(far["mats"][:1] + far["tp"] + far["mats"][1:] + near)
+    return layout, [one, two] if one != two else [one]
+
+
+def per_device(scale, digits, grad, momentum):
     new_momentum = momentum_beta * momentum + grad.astype(jnp.float32)
     iterate = (grad.astype(jnp.float32) + momentum_beta * new_momentum).astype(jnp.bfloat16)
-    columns = lax.all_gather(iterate, "tp", axis=0, tiled=True)
+    layout, orders = orders_of(digits)
+    lines = {axis: tuple(sorted(found, key=lambda d: d[3])) for axis, found in digits.items()}
+    columns = gather(iterate, "tp", tuple(digits["tp"]), [lines["tp"]], 6, 1, "gather_x")
     size = columns.shape[0]
     mine = iterate.shape[0]
     block = math.gcd(mine, 256)
@@ -172,7 +395,7 @@
         name="gram",
     )(tp.reshape(1), columns)
     share = lax.psum_scatter(part, "mats", scatter_dimension=0, tiled=True)
-    compact = lax.all_gather(share, ("tp", "mats"), axis=0, tiled=True)
+    compact = gather(share, ("tp", "mats"), layout, orders, 2, 2, "gather_gram")
     count = share.shape[0]
     place = tp * lax.axis_size("mats") + lax.axis_index("mats")
     thin = pltpu.VMEM((count, size), jnp.bfloat16)
@@ -191,17 +414,19 @@
         ),
         name="poly",
     )(place.reshape(1), compact)
-    matrix = lax.all_gather(rows, "mats", axis=0, tiled=True)
+    matrix = gather(rows, "mats", tuple(digits["mats"]), [lines["mats"]], 3, 3, "gather_rows")
     product = jnp.dot(matrix, columns, preferred_element_type=jnp.float32)
     update = (product + kappa[0, 0] * iterate.astype(jnp.float32)).astype(jnp.bfloat16)
     return (update, new_momentum)
 
 
 def solution(mesh):
+    digits = digits_of(mesh)
+
     def step(grad, momentum):
         scale = shape_gain * math.sqrt(max(grad.shape))
         return jax.shard_map(
-            functools.partial(per_device, scale),
+            functools.partial(per_device, scale, digits),
             mesh=mesh,
             in_specs=(P("tp", "mats"), P("tp", "mats")),
             out_specs=(P("tp", "mats"), P("tp", "mats")),

time: 429 us -> 370 us (0.86)
  waiting for transfers between devices: 325 us -> 72.9 us
  Pallas kernels: 63.4 us -> 256 us
    all_gather x3 -> x0, waiting for transfers between devices: 253 us -> none  [the longest x1 90.1 us: per_device(): compact = lax.all_gather(share, ('tp', 'mats'), axis=0, tiled=True)]
    pallas_call x0 -> x3, Pallas kernels: none -> 193 us  [gather(): pl.pallas_call(functools.partial(gather_kernel, layout, pieces), out_shap...]
  transfers between devices with their start and end apart: 4 -> 1, of which waited for: 4 -> 1; matrix products, arithmetic and copies ran while one was open for 0% -> 0% of each run, Pallas kernels for 0% -> 0%
where the time goes in v2:
time: 370 us; the launch traced here: 369 us
  Pallas kernels  256 us (69%)
  waiting for transfers between devices  72.9 us (20%)
  matrix products  16.8 us (5%)
  between operations  14.1 us (4%)
  other arithmetic  9.26 us (3%)
    pallas_call x3, Pallas kernels, gather(): pl.pallas_call(functools.partial(gather_kernel, layout, pieces), out_shap...  193 us
    reduce_scatter x1, waiting for transfers between devices, per_device(): share = lax.psum_scatter(part, 'mats', scatter_dimension=0, tiled=True)  72.9 us
    pallas_call x1, Pallas kernels, per_device(): pl.pallas_call(functools.partial(poly_kernel, block, scale), out_shape=(j...  51.6 us
    dot_general x1, matrix products, per_device(): product = jnp.dot(matrix, columns, preferred_element_type=jnp.float32)  16.8 us
    pallas_call x1, Pallas kernels, per_device(): pl.pallas_call(functools.partial(gram_kernel, block), out_shape=jax.Shape...  12 us
    convert_element_type x1, other arithmetic, per_device(): (grad.astype(jnp.float32) + momentum_beta * new_momentum).astype(jnp.bflo...  9.26 us
  transfers between devices with their start and end apart: 1, of which 1 were waited for; matrix products, arithmetic and copies ran while one was open for 0% of the time, Pallas kernels for 0%

profile of v2, /device:TPU:0, one launch (start us, length us, event | category | flops | bytes accessed | tf_op | source)
XLA Modules:
  0.0 369.3 jit_solution(11979485870550036438)
XLA Ops:
  7.2 0.0 reduce-scatter.2.cloned.1.call-start
  7.2 9.3 %fusion = (bf16[768,2048]{1,0:T(8,128)(2,1)}, f32[768,2048]{1,0:T(8,128)}) fusion(bf16[768,2048]{1,0:T(8,128)(2,1)} %param.2, f32[768,2048]{1,0:T(8,128)} %param.3), kind=kLoop, calls=%fused_computation.2 | loop fusion | flops 9437184 | bytes 18874368 | tf_op jit(solution)/shard_map/convert_element_type | solution.py:377
  16.5 78.2 %gather_x.1 = bf16[2,2,768,2048]{3,2,1,0:T(8,128)(2,1)} custom-call(bf16[768,2048]{1,0:T(8,128)(2,1)} %get-tuple-element.6.x_ref), custom_call_target="tpu_custom_call" | custom-call | tf_op jit(solution)/shard_map/gather_x/pallas_call | solution.py:220
  94.7 12.0 %gram.1 = bf16[768,1792]{1,0:T(8,128)(2,1)} custom-call(s32[1]{0:T(128)} %bitcast.1.where_ref, bf16[3072,2048]{1,0:T(8,128)(2,1)} %bitcast.9), custom_call_target="tpu_custom_call" | custom-call | tf_op jit(solution)/shard_map/gram/pallas_call | solution.py:389
  106.7 0.0 reduce-scatter.2.cloned.1.call-update
  106.7 72.9 %reduce-scatter.2.cloned.1.call-done.x_ref = bf16[96,1792]{1,0:T(8,128)(2,1)} async-done(((bf16[768,1792]{1,0:T(8,128)(2,1)}), bf16[96,1792]{1,0:T(8,128)(2,1)}) %reduce-scatter.2.cloned.1.call-update) | async-done | bytes 344080 | tf_op jit(solution)/shard_map/reduce_scatter | solution.py:397
  179.6 57.5 %gather_gram.1 = bf16[2,2,4,2,96,1792]{5,4,3,2,1,0:T(8,128)(2,1)} custom-call(bf16[96,1792]{1,0:T(8,128)(2,1)} %reduce-scatter.2.cloned.1.call-done.x_ref), custom_call_target="tpu_custom_call" | custom-call | tf_op jit(solution)/shard_map/gather_gram/pallas_call | solution.py:220
  237.1 51.6 %poly.1 = (bf16[96,3072]{1,0:T(8,128)(2,1)}, f32[1,128]{1,0:T(1,128)}) custom-call(s32[1]{0:T(128)} %bitcast.where_ref, bf16[3072,1792]{1,0:T(8,128)(2,1)} %bitcast.11), custom_call_target="tpu_custom_call" | custom-call | flops 19931332608 | bytes 11010048 | tf_op jit(solution)/shard_map/poly/pallas_call | solution.py:402
  288.7 57.0 %gather_rows.1 = bf16[4,2,96,3072]{3,2,1,0:T(8,128)(2,1)} custom-call(bf16[96,3072]{1,0:T(8,128)(2,1)} %get-tuple-element.4.x_ref), custom_call_target="tpu_custom_call" | custom-call | tf_op jit(solution)/shard_map/gather_rows/pallas_call | solution.py:220
  345.7 16.8 %add_convert_fusion = bf16[768,2048]{1,0:T(8,128)(2,1)} fusion(bf16[768,2048]{1,0:T(8,128)(2,1)} %get-tuple-element.6.x_ref, bf16[768,3072]{1,0:T(8,128)(2,1)} %bitcast.12, bf16[3072,2048]{1,0:T(8,128)(2,1)} %bitcast.10, f32[]{:T(128)} %bitcast.13), kind=kOutput, calls=%fused_computation.3 | convolution fusion | flops 9669967872 | bytes 23592964 | tf_op jit(solution)/shard_map/dot_general | solution.py:418
Async XLA Ops:
  7.2 172.5 %reduce-scatter.2.cloned.1.call-start = ((), (), s32[]{:S(2)}) async-start(), calls=%async_computation.1 | async-start | bytes 3096576 | tf_op jit(solution)/shard_map/reduce_scatter | solution.py:397
Sparse Core Ops, SparseCore 0:
  106.8 72.7 reduce-scatter.1

commit v3 on v2

--- a/solution.py
+++ b/solution.py
@@ -81,10 +81,30 @@
     pl.semaphore_wait(semaphore, count)
 
 
+def around(digit, step):
+    here = place(digit)
+    there = lax.rem(here + step, digit[2])
+    return there, there - here
+
+
+def barrier_lines(digits):
+    semaphore = pltpu.get_barrier_semaphore()
+    count = 0
+    for digit in digits:
+        for step in range(1, digit[2]):
+            _, offset = around(digit, step)
+            pl.semaphore_signal(
+                semaphore, inc=1, device_id=peer(digit, offset),
+                device_id_type=pl.DeviceIdType.MESH,
+            )
+            count += 1
+    pl.semaphore_wait(semaphore, count)
+
+
 def relatives(digit):
     here, extent = place(digit), digit[2]
     if extent == 2:
-        return [(1, 2 * here - 1, 1 - here, None)]
+        return [(1, 0, 1 - here, None)]
     found = []
     for hop in range(1, extent):
         found.append((hop, 1, here - hop, here >= hop))
@@ -96,7 +116,7 @@
     def __init__(self, layout, pieces, buffer, source, send_sem, recv_sem):
         self.layout, self.pieces, self.buffer, self.source = layout, pieces, buffer, source
         self.send_sem, self.recv_sem = send_sem, recv_sem
-        self.sent = []
+        self.sent = {}
 
     @staticmethod
     def semaphores(layout, pieces):
@@ -121,14 +141,14 @@
             device_id_type=pl.DeviceIdType.MESH,
         )
 
-    def send(self, piece, block, exists, digit, directions, own=False):
+    def send(self, piece, block, exists, digit, directions, tag, own=False):
         for way, (offset, has) in enumerate(moves(digit)):
             if directions is not None and way not in directions:
                 continue
             copy = self.copy(piece, block, digit, offset, way, own)
             condition = both(exists, has)
             when(condition, copy.start)
-            self.sent.append((condition, copy))
+            self.sent[(piece, tag, digit, way)] = (block, exists, own)
 
     def events(self, piece):
         order = self.pieces[piece][0]
@@ -137,52 +157,62 @@
 
         def begin(after):
             for digit in order:
-                self.send(piece, here, None, digit, None, own=True)
-
-        found.append((0, begin))
-
-        def arrivals(stage, block, exists, depth):
+                self.send(piece, here, None, digit, None, (), own=True)
+
+        found.append((0, begin, ()))
+
+        def arrivals(stage, block, exists, tag, depth):
             digit = order[stage]
             for hop, travel, q, there in relatives(digit):
                 source = {**block, digit: q}
                 condition = both(exists, there)
-
-                def arrive(after, stage=stage, digit=digit, source=source, condition=condition, hop=hop, travel=travel):
+                label = tag + ((digit, hop, travel),)
+
+                def arrive(after, source=source, condition=condition, travel=travel, label=label):
                     offset, _ = moves(digit)[0]
                     when(condition, self.copy(piece, source, digit, offset, 0, False).wait_recv)
                     if digit[2] > 2:
-                        self.send(piece, source, condition, digit, (0 if travel > 0 else 1,))
+                        self.send(piece, source, condition, digit, (0 if travel > 0 else 1,), label)
                     for later in order[stage + 1 :]:
-                        self.send(piece, source, condition, later, None)
+                        self.send(piece, source, condition, later, None, label)
                     if after is not None:
-                        after(piece, source, condition)
-
-                found.append((depth + hop, arrive))
-
-        def expand(stage, earlier, block, exists, depth):
+                        after(piece, source, condition, label)
+
+                found.append((depth + hop, arrive, label))
+
+        def expand(stage, earlier, block, exists, tag, depth):
             if earlier == stage:
-                arrivals(stage, block, exists, depth)
+                arrivals(stage, block, exists, tag, depth)
                 return
             digit = order[earlier]
-            expand(stage, earlier + 1, {**block, digit: here[digit]}, exists, depth)
-            for hop, _, q, there in relatives(digit):
-                expand(stage, earlier + 1, {**block, digit: q}, both(exists, there), depth + hop)
+            expand(stage, earlier + 1, {**block, digit: here[digit]}, exists, tag, depth)
+            for hop, travel, q, there in relatives(digit):
+                expand(
+                    stage, earlier + 1, {**block, digit: q}, both(exists, there),
+                    tag + ((digit, hop, travel),), depth + hop,
+                )
 
         for stage in range(len(order)):
-            expand(stage, 0, dict(here), None, 0)
+            expand(stage, 0, dict(here), None, (), 0)
         return found
 
+    def queue(self):
+        entries = []
+        for piece in range(len(self.pieces)):
+            for depth, action, tag in self.events(piece):
+                entries.append((depth, piece, len(entries), action, tag))
+        entries.sort(key=lambda entry: entry[:3])
+        return [(piece, action, tag) for _, piece, _, action, tag in entries]
+
     def run(self, after=None):
-        queue = []
-        for piece in range(len(self.pieces)):
-            for depth, action in self.events(piece):
-                queue.append((depth, piece, len(queue), action))
-        for _, _, _, action in sorted(queue, key=lambda entry: entry[:3]):
+        for _, action, _ in self.queue():
             action(after)
 
     def drain(self):
-        for condition, copy in self.sent:
-            when(condition, copy.wait_send)
+        for (piece, _, digit, way), (block, exists, own) in self.sent.items():
+            offset, has = moves(digit)[way]
+            copy = self.copy(piece, block, digit, offset, way, own)
+            when(both(exists, has), copy.wait_send)
 
 
 def gather_kernel(layout, pieces, x_ref, out_ref, send_sem, recv_sem, local_sem):
@@ -260,6 +290,202 @@
             )
 
 
+def reduce_kernel(
+    block, rows, pieces, far, near, x_ref, columns_ref, share_ref, held, part, got_near, half, got_far,
+    send_sem, recv_sem, near_send, near_recv, far_send, far_recv, out_sem,
+):
+    order = pieces[0][0]
+    layout = tuple(sorted(order, key=lambda d: -d[1]))
+    shards = math.prod(d[2] for d in layout)
+    mine = x_ref.shape[0] // block
+    window = part.shape[0]
+    lines = far[2]
+    axis = layout[0][0]
+    shard = lax.axis_index(axis)
+    barrier_lines(layout + (far, near))
+    gather = Gather(layout, pieces, held, x_ref, send_sem, recv_sem)
+    queue = gather.queue()
+    starts = [entry for entry in queue if not entry[2]]
+    events = [entry for entry in queue if entry[2]]
+
+    def home(t, tag):
+        for digit, _, _ in tag:
+            _, stride, _, _ = digit
+            t = t - stride if (t // stride) % 2 else t + stride
+        return t
+
+    def needed(t, d):
+        wanted = set()
+        for i in range(mine):
+            s, piece = (i + d) // mine % shards, (i + d) % mine
+            if s:
+                wanted.add(((t + s) % shards, piece))
+        return wanted
+
+    slots = [[] for _ in range(window + 1)]
+    done = [0] * shards
+    for d in range(window + 1):
+        begun = {}
+        for t in range(shards):
+            last = len(events)
+            if d < window:
+                wanted = needed(t, d)
+                last = max(
+                    [done[t]]
+                    + [e + 1 for e, (piece, _, tag) in enumerate(events) if (home(t, tag), piece) in wanted]
+                )
+            for e in range(done[t], last):
+                begun.setdefault(e, []).append(t)
+            done[t] = last
+        slots[d] = sorted(begun.items())
+
+    copies = {}
+
+    def keep(piece, source, condition, tag):
+        _, row, count = pieces[piece]
+        at = tuple(source[d] for d in layout) + (pl.ds(row, count), slice(None))
+        number = next(e for e, entry in enumerate(events) if entry[0] == piece and entry[2] == tag)
+        copies[number] = at
+        pltpu.make_async_copy(held.at[at], columns_ref.at[at], out_sem.at[number]).start()
+
+    for _, action, _ in starts:
+        action(None)
+    own = pltpu.make_async_copy(
+        x_ref, columns_ref.at[tuple(place(d) for d in layout)], out_sem.at[len(events)]
+    )
+    own.start()
+
+    def advance(d):
+        for e, who in slots[d]:
+            _, action, _ = events[e]
+            if len(who) == shards:
+                action(keep)
+            else:
+                condition = functools.reduce(lambda a, b: a | b, [shard == t for t in who])
+                pl.when(condition)(functools.partial(action, keep))
+
+    def owner_rows(far_place, near_place):
+        start = (far_place * far[1] + near_place * near[1]) * rows
+        return pl.ds(pl.multiple_of(start, 16), rows)
+
+    def near_copy(d, line):
+        return pltpu.make_async_remote_copy(
+            src_ref=part.at[d, owner_rows(line, 1 - place(near)), :],
+            dst_ref=got_near.at[d, line],
+            send_sem=near_send.at[d, line],
+            recv_sem=near_recv.at[d, line],
+            device_id=peer(near, 1 - 2 * place(near)),
+            device_id_type=pl.DeviceIdType.MESH,
+        )
+
+    def far_copy(d, step, arriving):
+        there, offset = around(far, step)
+        slot = there if arriving else place(far)
+        return pltpu.make_async_remote_copy(
+            src_ref=half.at[d, there],
+            dst_ref=got_far.at[d, slot],
+            send_sem=far_send.at[d, there],
+            recv_sem=far_recv.at[d, slot],
+            device_id=peer(far, offset),
+            device_id_type=pl.DeviceIdType.MESH,
+        )
+
+    def form(d):
+        for i in range(mine):
+            s, piece = (i + d) // mine % shards, (i + d) % mine
+            at = (pl.ds(piece * block, block), slice(None))
+            if s:
+                other = lax.rem(shard + s, shards)
+                at = tuple(lax.rem(lax.div(other, g[1]), g[2]) for g in layout) + at
+                right = held[at]
+            else:
+                right = x_ref[at]
+            left = x_ref[i * block : (i + 1) * block, :]
+            part[d, i * block : (i + 1) * block, :] = nt_dot(left, right).astype(jnp.bfloat16)
+        for line in range(lines):
+            near_copy(d, line).start()
+
+    def halve(d):
+        for line in range(lines):
+            near_copy(d, line).wait_recv()
+            half[d, line] = (
+                part[d, owner_rows(line, place(near)), :].astype(jnp.float32)
+                + got_near[d, line].astype(jnp.float32)
+            ).astype(jnp.bfloat16)
+        for step in range(1, lines):
+            far_copy(d, step, False).start()
+
+    def finish(d):
+        total = half[d, place(far)].astype(jnp.float32)
+        for step in range(1, lines):
+            there, _ = around(far, step)
+            far_copy(d, step, True).wait_recv()
+            total = total + got_far[d, there].astype(jnp.float32)
+        share_ref[:, d * block : (d + 1) * block] = total.astype(jnp.bfloat16)
+
+    for d in range(window + 2):
+        if d <= window:
+            if d > 0:
+                halve(d - 1)
+            if d > 1:
+                finish(d - 2)
+            advance(d)
+        else:
+            finish(d - 2)
+        if d < window:
+            form(d)
+
+    for d in range(window):
+        for line in range(lines):
+            near_copy(d, line).wait_send()
+        for step in range(1, lines):
+            far_copy(d, step, False).wait_send()
+    for number, at in copies.items():
+        pltpu.make_async_copy(held.at[at], columns_ref.at[at], out_sem.at[number]).wait()
+    own.wait()
+    gather.drain()
+
+
+def reduced_gram(iterate, digits, block, window, ident):
+    layout = tuple(digits["tp"])
+    if len(digits["mats"]) != 2 or any(d[2] != 2 for d in layout):
+        return None
+    far, near = digits["mats"]
+    mine, width = iterate.shape
+    rows = mine // (far[2] * near[2])
+    if near[2] != 2 or rows % 16 or mine % block:
+        return None
+    order = tuple(sorted(layout, key=lambda d: d[3]))
+    pieces = [(order, row, block) for row in range(0, mine, block)]
+    dims = tuple(d[2] for d in layout)
+    chunks, lines = window // block, far[2]
+    tile = pltpu.VMEM((chunks, lines, rows, block), jnp.bfloat16)
+    dma = pltpu.SemaphoreType.DMA
+    blocks = math.prod(dims) - 1
+    columns, share = pl.pallas_call(
+        functools.partial(reduce_kernel, block, rows, pieces, far, near),
+        out_shape=(
+            jax.ShapeDtypeStruct(dims + iterate.shape, jnp.bfloat16),
+            jax.ShapeDtypeStruct((rows, window), jnp.bfloat16),
+        ),
+        in_specs=[pl.BlockSpec(memory_space=pltpu.VMEM)],
+        out_specs=(pl.BlockSpec(memory_space=pl.ANY), pl.BlockSpec(memory_space=pltpu.VMEM)),
+        scratch_shapes=[
+            pltpu.VMEM(dims + iterate.shape, jnp.bfloat16),
+            pltpu.VMEM((chunks, mine, block), jnp.bfloat16),
+            tile, tile, tile,
+        ]
+        + Gather.semaphores(layout, pieces)
+        + [dma((chunks, lines))] * 4
+        + [dma((blocks * len(pieces) + 1,))],
+        compiler_params=pltpu.CompilerParams(
+            collective_id=ident, has_side_effects=True, vmem_limit_bytes=grant
+        ),
+        name="reduced_gram",
+    )(iterate)
+    return columns.reshape(dims[0] * math.prod(dims[1:]) * mine, width), share
+
+
 def poly_kernel(block, scale, where_ref, compact_ref, out_ref, kappa_ref, gram, own, one, two, left, right):
     size = gram.shape[0]
     blocks = size // block
@@ -377,8 +603,7 @@
     iterate = (grad.astype(jnp.float32) + momentum_beta * new_momentum).astype(jnp.bfloat16)
     layout, orders = orders_of(digits)
     lines = {axis: tuple(sorted(found, key=lambda d: d[3])) for axis, found in digits.items()}
-    columns = gather(iterate, "tp", tuple(digits["tp"]), [lines["tp"]], 6, 1, "gather_x")
-    size = columns.shape[0]
+    size = momentum.shape[0] * lax.axis_size("tp")
     mine = iterate.shape[0]
     block = math.gcd(mine, 256)
     window = window_of(size // block) * block
@@ -386,15 +611,20 @@
     whole = pl.BlockSpec(memory_space=pltpu.VMEM)
     params = pltpu.CompilerParams(vmem_limit_bytes=grant)
     tp = lax.axis_index("tp")
-    part = pl.pallas_call(
-        functools.partial(gram_kernel, block),
-        out_shape=jax.ShapeDtypeStruct((mine, window), jnp.bfloat16),
-        in_specs=[smem, whole],
-        out_specs=whole,
-        compiler_params=params,
-        name="gram",
-    )(tp.reshape(1), columns)
-    share = lax.psum_scatter(part, "mats", scatter_dimension=0, tiled=True)
+    fused = reduced_gram(iterate, digits, block, window, 1)
+    if fused is not None:
+        columns, share = fused
+    else:
+        columns = gather(iterate, "tp", tuple(digits["tp"]), [lines["tp"]], 6, 1, "gather_x")
+        part = pl.pallas_call(
+            functools.partial(gram_kernel, block),
+            out_shape=jax.ShapeDtypeStruct((mine, window), jnp.bfloat16),
+            in_specs=[smem, whole],
+            out_specs=whole,
+            compiler_params=params,
+            name="gram",
+        )(tp.reshape(1), columns)
+        share = lax.psum_scatter(part, "mats", scatter_dimension=0, tiled=True)
     compact = gather(share, ("tp", "mats"), layout, orders, 2, 2, "gather_gram")
     count = share.shape[0]
     place = tp * lax.axis_size("mats") + lax.axis_index("mats")

time: 370 us -> 305 us (0.82)
  waiting for transfers between devices: 72.9 us -> 0 us
  Pallas kernels: 256 us -> 278 us
  between operations: 14.1 us -> 0.66 us
    pallas_call x1, Pallas kernels: 12 us -> 107 us  [reduced_gram(): pl.pallas_call(functools.partial(reduce_kernel, block, rows, pieces, far,...]
    reduce_scatter x1 -> x0, waiting for transfers between devices: 72.9 us -> none  [per_device(): share = lax.psum_scatter(part, 'mats', scatter_dimension=0, tiled=True)]
    pallas_call x3 -> x2, Pallas kernels: 193 us -> 120 us  [gather(): pl.pallas_call(functools.partial(gather_kernel, layout, pieces), out_shap...]
  transfers between devices with their start and end apart: 1 -> 0, of which waited for: 1 -> 0; matrix products, arithmetic and copies ran while one was open for 0% -> 0% of each run, Pallas kernels for 0% -> 0%
where the time goes in v3:
time: 305 us
  Pallas kernels  278 us (91%)
  matrix products  16.8 us (6%)
  other arithmetic  9.26 us (3%)
    pallas_call x2, Pallas kernels, gather(): pl.pallas_call(functools.partial(gather_kernel, layout, pieces), out_shap...  120 us
    pallas_call x1, Pallas kernels, reduced_gram(): pl.pallas_call(functools.partial(reduce_kernel, block, rows, pieces, far,...  107 us
    pallas_call x1, Pallas kernels, per_device(): pl.pallas_call(functools.partial(poly_kernel, block, scale), out_shape=(j...  51.5 us
    dot_general x1, matrix products, per_device(): product = jnp.dot(matrix, columns, preferred_element_type=jnp.float32)  16.8 us
    convert_element_type x1, other arithmetic, per_device(): (grad.astype(jnp.float32) + momentum_beta * new_momentum).astype(jnp.bflo...  9.26 us

profile of v3, /device:TPU:0, one launch (start us, length us, event | category | flops | bytes accessed | tf_op | source)
XLA Modules:
  0.0 304.8 jit_solution(1671964133861616918)
XLA Ops:
  0.6 9.3 %fusion = (bf16[768,2048]{1,0:T(8,128)(2,1)}, f32[768,2048]{1,0:T(8,128)}) fusion(bf16[768,2048]{1,0:T(8,128)(2,1)} %param.2, f32[768,2048]{1,0:T(8,128)} %param.3), kind=kLoop, calls=%fused_computation.2 | loop fusion | flops 9437184 | bytes 18874368 | tf_op jit(solution)/shard_map/convert_element_type | solution.py:603
  9.9 106.8 %reduced_gram.1 = (bf16[2,2,768,2048]{3,2,1,0:T(8,128)(2,1)}, bf16[96,1792]{1,0:T(8,128)(2,1)}) custom-call(bf16[768,2048]{1,0:T(8,128)(2,1)} %get-tuple-element.10.x_ref), custom_call_target="tpu_custom_call" | custom-call | tf_op jit(solution)/shard_map/reduced_gram/pallas_call | solution.py:465
  116.7 63.1 %gather_gram.1 = bf16[2,2,4,2,96,1792]{5,4,3,2,1,0:T(8,128)(2,1)} custom-call(bf16[96,1792]{1,0:T(8,128)(2,1)} %get-tuple-element.6.x_ref), custom_call_target="tpu_custom_call" | custom-call | tf_op jit(solution)/shard_map/gather_gram/pallas_call | solution.py:250
  179.9 51.5 %poly.1 = (bf16[96,3072]{1,0:T(8,128)(2,1)}, f32[1,128]{1,0:T(1,128)}) custom-call(s32[1]{0:T(128)} %bitcast.where_ref, bf16[3072,1792]{1,0:T(8,128)(2,1)} %bitcast.8), custom_call_target="tpu_custom_call" | custom-call | flops 19931332608 | bytes 11010048 | tf_op jit(solution)/shard_map/poly/pallas_call | solution.py:632
  231.3 56.7 %gather_rows.1 = bf16[4,2,96,3072]{3,2,1,0:T(8,128)(2,1)} custom-call(bf16[96,3072]{1,0:T(8,128)(2,1)} %get-tuple-element.7.x_ref), custom_call_target="tpu_custom_call" | custom-call | tf_op jit(solution)/shard_map/gather_rows/pallas_call | solution.py:250
  288.0 16.8 %add_convert_fusion = bf16[768,2048]{1,0:T(8,128)(2,1)} fusion(bf16[768,2048]{1,0:T(8,128)(2,1)} %get-tuple-element.10.x_ref, bf16[768,3072]{1,0:T(8,128)(2,1)} %bitcast.9, bf16[3072,2048]{1,0:T(8,128)(2,1)} %bitcast.10, f32[]{:T(128)} %bitcast.11), kind=kOutput, calls=%fused_computation.3 | convolution fusion | flops 9669967872 | bytes 23592964 | tf_op jit(solution)/shard_map/dot_general | solution.py:648

commit v4 on v3

--- a/solution.py
+++ b/solution.py
@@ -486,6 +486,103 @@
     return columns.reshape(dims[0] * math.prod(dims[1:]) * mine, width), share
 
 
+def polynomial_rows(gram, own, one, two, left, right, scale, where_ref):
+    size = gram.shape[0]
+
+    def column_sums(step, total):
+        rows = jnp.abs(gram[pl.ds(pl.multiple_of(step * 16, 16), 16), :].astype(jnp.float32))
+        return total + (rows[0:8] + rows[8:16])
+
+    total = lax.fori_loop(0, size // 16, column_sums, jnp.zeros((8, size), jnp.float32))
+    bound = jnp.max(jnp.sum(total, axis=0, keepdims=True), axis=1, keepdims=True) + epsilon
+    root = lax.rsqrt(jnp.broadcast_to(bound, (1, 128)))
+    inverse = (root * root)[:, :1]
+    count = own.shape[0]
+    width = math.gcd(size, 1024)
+    if where_ref is None:
+        index = lax.axis_index("tp") * lax.axis_size("mats") + lax.axis_index("mats")
+    else:
+        index = where_ref[0]
+
+    def columns(body):
+        @pl.loop(0, size // width)
+        def _(step):
+            body(pl.ds(pl.multiple_of(step * width, width), width))
+
+    def times_gram(source, at):
+        return inverse * jnp.dot(source[...], gram[:, at], preferred_element_type=jnp.float32)
+
+    def wide(ref, at):
+        return ref[:, at].astype(jnp.float32)
+
+    def apply(source, target, constant=None):
+        def body(at):
+            value = times_gram(source, at)
+            if constant is not None:
+                value = value + (constant * inverse) * wide(own, at)
+            target[:, at] = value.astype(jnp.bfloat16)
+
+        columns(body)
+
+    def polynomial(source, middle, target):
+        apply(source, middle)
+
+        def body(at):
+            target[:, at] = (
+                first_coef * wide(source, at)
+                + second_coef * wide(middle, at)
+                + third_coef * times_gram(middle, at)
+            ).astype(jnp.bfloat16)
+
+        columns(body)
+
+    if count % 16 == 0:
+        own[...] = gram[pl.ds(pl.multiple_of(index * count, 16), count), :]
+    else:
+        row = lax.broadcasted_iota(jnp.int32, (count, size), 0) + index * count
+        column = lax.broadcasted_iota(jnp.int32, (count, size), 1)
+        two[...] = (row == column).astype(jnp.float32).astype(jnp.bfloat16)
+
+        def select(at):
+            own[:, at] = jnp.dot(
+                two[...], gram[:, at], preferred_element_type=jnp.float32
+            ).astype(jnp.bfloat16)
+
+        columns(select)
+
+    def start(at):
+        left[:, at] = (inverse * wide(own, at)).astype(jnp.bfloat16)
+
+    columns(start)
+
+    def first(at):
+        one[:, at] = (
+            second_coef * wide(left, at) + third_coef * times_gram(left, at)
+        ).astype(jnp.bfloat16)
+
+    columns(first)
+    apply(one, left, first_coef)
+    polynomial(left, right, two)
+    polynomial(two, right, left)
+
+    def keep(at):
+        two[:, at] = left[:, at]
+
+    columns(keep)
+    apply(two, right)
+    polynomial(right, left, own)
+    polynomial(own, left, right)
+
+    def finish(at):
+        mixed = (
+            first_coef * wide(one, at) + second_coef * wide(two, at) + third_coef * wide(right, at)
+        )
+        left[:, at] = ((scale * root[:, :1]) * mixed).astype(jnp.bfloat16)
+
+    columns(finish)
+    return root
+
+
 def poly_kernel(block, scale, where_ref, compact_ref, out_ref, kappa_ref, gram, own, one, two, left, right):
     size = gram.shape[0]
     blocks = size // block
@@ -498,95 +595,145 @@
             if d > 0 and 2 * d != blocks:
                 gram[j * block : (j + 1) * block, i * block : (i + 1) * block] = tile.T
 
-    def column_sums(step, total):
-        rows = jnp.abs(gram[pl.ds(pl.multiple_of(step * 16, 16), 16), :].astype(jnp.float32))
-        return total + (rows[0:8] + rows[8:16])
-
-    total = lax.fori_loop(0, size // 16, column_sums, jnp.zeros((8, size), jnp.float32))
-    bound = jnp.max(jnp.sum(total, axis=0, keepdims=True), axis=1, keepdims=True) + epsilon
-    root = lax.rsqrt(jnp.broadcast_to(bound, (1, 128)))
-    kappa = (scale * first_coef * first_coef) * root
-    kappa_ref[...] = kappa
-    inverse = (root * root)[:, :1]
-    count = own.shape[0]
-    width = math.gcd(size, 1024)
-
-    def columns(body):
-        @pl.loop(0, size // width)
+    root = polynomial_rows(gram, own, one, two, left, right, scale, where_ref)
+    kappa_ref[...] = (scale * first_coef * first_coef) * root
+    out_ref[...] = left[...]
+
+
+def finish_kernel(
+    block, scale, layout, pieces, near_pieces, share_ref, columns_ref, out_ref, held, gram, own, one, two, left,
+    right, rows, columns, result, send_sem, recv_sem, rows_send, rows_recv, in_sem, out_sem,
+):
+    barrier_all(layout)
+    tp = tuple(d for d in layout if d[0] == "tp")
+    far, near = (d for d in layout if d[0] == "mats")
+    load = pltpu.make_async_copy(columns_ref, columns, in_sem)
+    gather = Gather(layout, pieces, held, share_ref, send_sem, recv_sem)
+    queue = gather.queue()
+    for _, action, tag in queue:
+        if not tag:
+            action(None)
+    load.start()
+    held[tuple(place(d) for d in layout)] = share_ref[...]
+    for _, action, tag in queue:
+        if tag:
+            action(None)
+
+    size = gram.shape[0]
+    count, window = share_ref.shape
+    blocks = size // block
+    shards = math.prod(d[2] for d in tp)
+    mine = size // shards
+    for t in range(shards):
+        at = tuple((t // d[1]) % d[2] for d in tp)
+        for d in range(window // block):
+            strip = held[at + (slice(None), slice(None), slice(None), pl.ds(d * block, block))]
+            strip = strip.reshape(mine, block)
+            for k in range(mine // block):
+                i = t * (mine // block) + k
+                j = (i + d) % blocks
+                tile = strip[k * block : (k + 1) * block, :]
+                gram[i * block : (i + 1) * block, j * block : (j + 1) * block] = tile
+                if d > 0 and 2 * d != blocks:
+                    gram[j * block : (j + 1) * block, i * block : (i + 1) * block] = tile.T
+
+    root = polynomial_rows(gram, own, one, two, left, right, scale, None)
+    kappa = ((scale * first_coef * first_coef) * root)[:, :1]
+
+    spread = Gather((far, near), near_pieces, rows, left, rows_send, rows_recv)
+    queue = spread.queue()
+    for _, action, tag in queue:
+        if not tag:
+            action(None)
+    rows[place(far), place(near)] = left[...]
+    load.wait()
+    pair = near[2] * count
+    width = math.gcd(columns.shape[1], 512)
+    shard_row = lax.axis_index("tp") * mine
+
+    def multiply(line):
+        matrix = rows[line].reshape(pair, size)
+        at = pl.ds(pl.multiple_of(line * pair, 16), pair)
+        mirror = pl.ds(pl.multiple_of(shard_row + line * pair, 16), pair)
+
+        @pl.loop(0, columns.shape[1] // width)
         def _(step):
-            body(pl.ds(pl.multiple_of(step * width, width), width))
-
-    def times_gram(source, at):
-        return inverse * jnp.dot(source[...], gram[:, at], preferred_element_type=jnp.float32)
-
-    def wide(ref, at):
-        return ref[:, at].astype(jnp.float32)
-
-    def apply(source, target, constant=None):
-        def body(at):
-            value = times_gram(source, at)
-            if constant is not None:
-                value = value + (constant * inverse) * wide(own, at)
-            target[:, at] = value.astype(jnp.bfloat16)
-
-        columns(body)
-
-    def polynomial(source, middle, target):
-        apply(source, middle)
-
-        def body(at):
-            target[:, at] = (
-                first_coef * wide(source, at)
-                + second_coef * wide(middle, at)
-                + third_coef * times_gram(middle, at)
+            across = pl.ds(pl.multiple_of(step * width, width), width)
+            product = jnp.dot(matrix, columns[:, across], preferred_element_type=jnp.float32)
+            result[at, across] = (
+                product + kappa * columns[mirror, across].astype(jnp.float32)
             ).astype(jnp.bfloat16)
 
-        columns(body)
-
-    if count % 16 == 0:
-        own[...] = gram[pl.ds(pl.multiple_of(where_ref[0] * count, 16), count), :]
-    else:
-        row = lax.broadcasted_iota(jnp.int32, (count, size), 0) + where_ref[0] * count
-        column = lax.broadcasted_iota(jnp.int32, (count, size), 1)
-        two[...] = (row == column).astype(jnp.float32).astype(jnp.bfloat16)
-
-        def select(at):
-            own[:, at] = jnp.dot(
-                two[...], gram[:, at], preferred_element_type=jnp.float32
-            ).astype(jnp.bfloat16)
-
-        columns(select)
-
-    def start(at):
-        left[:, at] = (inverse * wide(own, at)).astype(jnp.bfloat16)
-
-    columns(start)
-
-    def first(at):
-        one[:, at] = (
-            second_coef * wide(left, at) + third_coef * times_gram(left, at)
-        ).astype(jnp.bfloat16)
-
-    columns(first)
-    apply(one, left, first_coef)
-    polynomial(left, right, two)
-    polynomial(two, right, left)
-
-    def keep(at):
-        two[:, at] = left[:, at]
-
-    columns(keep)
-    apply(two, right)
-    polynomial(right, left, own)
-    polynomial(own, left, right)
-
-    def finish(at):
-        mixed = (
-            first_coef * wide(one, at) + second_coef * wide(two, at) + third_coef * wide(right, at)
-        )
-        out_ref[:, at] = ((scale * root[:, :1]) * mixed).astype(jnp.bfloat16)
-
-    columns(finish)
+        pltpu.make_async_copy(result.at[at], out_ref.at[at], out_sem.at[line]).start()
+
+    groups = [(None, place(far), None)]
+    groups += [((far, hop, travel), q, there) for hop, travel, q, there in relatives(far)]
+    missing = []
+    for label, q, there in groups:
+        wanted = set()
+        for piece, _, tag in queue:
+            if tag and [part for part in tag if part[0] == far] == ([label] if label else []):
+                wanted.add((piece, tag))
+        missing.append((wanted, q, there))
+    for piece, action, tag in queue:
+        if not tag:
+            continue
+        action(None)
+        for wanted, q, there in missing:
+            if (piece, tag) in wanted:
+                wanted.remove((piece, tag))
+                if not wanted:
+                    when(there, functools.partial(multiply, q))
+    for line in range(far[2]):
+        at = pl.ds(line * pair, pair)
+        pltpu.make_async_copy(result.at[at], out_ref.at[at], out_sem.at[line]).wait()
+    gather.drain()
+    spread.drain()
+
+
+def finished(share, columns, digits, block, scale, ident):
+    layout, _ = orders_of(digits)
+    count, window = share.shape
+    if len(digits["mats"]) != 2 or len(digits["tp"]) != 2 or digits["mats"][1][2] != 2 or count % 16:
+        return None
+    far, near = digits["mats"]
+    side = [d for d in digits["tp"] if not d[3]]
+    close = tuple(d for d in digits["tp"] if d[3])
+    if len(side) != 1 or any(d[2] != 2 for d in digits["tp"]):
+        return None
+    orders = [(far, near, side[0]) + close, (far, side[0], near) + close]
+    pieces = pieces_of(count, orders, 2)
+    most = (count * 5 // 6 + 15) // 16 * 16
+    near_pieces = [((far, near), 0, most)]
+    if most < count:
+        near_pieces.append(((near, far), most, count - most))
+    size, width = columns.shape
+    dims = tuple(d[2] for d in layout)
+    mine = count * far[2] * near[2]
+    thin = pltpu.VMEM((count, size), jnp.bfloat16)
+    return pl.pallas_call(
+        functools.partial(finish_kernel, block, scale, layout, pieces, near_pieces),
+        out_shape=jax.ShapeDtypeStruct((mine, width), jnp.bfloat16),
+        in_specs=[pl.BlockSpec(memory_space=pltpu.VMEM), pl.BlockSpec(memory_space=pl.ANY)],
+        out_specs=pl.BlockSpec(memory_space=pl.ANY),
+        scratch_shapes=[
+            pltpu.VMEM(dims + share.shape, jnp.bfloat16),
+            pltpu.VMEM((size, size), jnp.bfloat16),
+        ]
+        + [thin] * 5
+        + [
+            pltpu.VMEM((far[2], near[2], count, size), jnp.bfloat16),
+            pltpu.VMEM((size, width), jnp.bfloat16),
+            pltpu.VMEM((mine, width), jnp.bfloat16),
+        ]
+        + Gather.semaphores(layout, pieces)
+        + Gather.semaphores((far, near), near_pieces)
+        + [pltpu.SemaphoreType.DMA, pltpu.SemaphoreType.DMA((far[2],))],
+        compiler_params=pltpu.CompilerParams(
+            collective_id=ident, has_side_effects=True, vmem_limit_bytes=63 * 1024 * 1024
+        ),
+        name="finished",
+    )(share, columns)
 
 
 def orders_of(digits):
@@ -625,6 +772,10 @@
             name="gram",
         )(tp.reshape(1), columns)
         share = lax.psum_scatter(part, "mats", scatter_dimension=0, tiled=True)
+    if fused is not None:
+        update = finished(share, columns, digits, block, scale, 2)
+        if update is not None:
+            return (update, new_momentum)
     compact = gather(share, ("tp", "mats"), layout, orders, 2, 2, "gather_gram")
     count = share.shape[0]
     place = tp * lax.axis_size("mats") + lax.axis_index("mats")

time: 305 us -> 286 us (0.938)
  matrix products: 16.8 us -> 0 us
  Pallas kernels: 278 us -> 272 us
  local copies, waits for them, and re-layouts: 0 us -> 3.97 us
    dot_general x1 -> x0, matrix products: 16.8 us -> none  [per_device(): product = jnp.dot(matrix, columns, preferred_element_type=jnp.float32)]
    pallas_call x3 -> x1, Pallas kernels: 171 us -> 165 us  [finished(): pl.pallas_call(functools.partial(finish_kernel, block, scale, layout, pie...]
    unnamed x0 -> x1, local copies, waits for them, and re-layouts: none -> 3.97 us
where the time goes in v4:
time: 286 us; the launch traced here: 285 us
  Pallas kernels  272 us (95%)
  other arithmetic  9.26 us (3%)
  local copies, waits for them, and re-layouts  3.97 us (1%)
    pallas_call x1, Pallas kernels, finished(): pl.pallas_call(functools.partial(finish_kernel, block, scale, layout, pie...  165 us
    pallas_call x1, Pallas kernels, reduced_gram(): pl.pallas_call(functools.partial(reduce_kernel, block, rows, pieces, far,...  107 us
    convert_element_type x1, other arithmetic, per_device(): (grad.astype(jnp.float32) + momentum_beta * new_momentum).astype(jnp.bflo...  9.26 us

profile of v4, /device:TPU:0, one launch (start us, length us, event | category | flops | bytes accessed | tf_op | source)
XLA Modules:
  0.0 285.5 jit_solution(10575478556122366156)
XLA Ops:
  0.6 9.3 %fusion = (bf16[768,2048]{1,0:T(8,128)(2,1)}, f32[768,2048]{1,0:T(8,128)}) fusion(bf16[768,2048]{1,0:T(8,128)(2,1)} %param.2, f32[768,2048]{1,0:T(8,128)} %param.3), kind=kLoop, calls=%fused_computation.2 | loop fusion | flops 9437184 | bytes 18874368 | tf_op jit(solution)/shard_map/convert_element_type | solution.py:750
  9.9 106.8 %reduced_gram.1 = (bf16[2,2,768,2048]{3,2,1,0:T(8,128)(2,1)}, bf16[96,1792]{1,0:T(8,128)(2,1)}) custom-call(bf16[768,2048]{1,0:T(8,128)(2,1)} %get-tuple-element.6.x_ref), custom_call_target="tpu_custom_call" | custom-call | tf_op jit(solution)/shard_map/reduced_gram/pallas_call | solution.py:465
  116.7 164.8 %finished.1 = bf16[768,2048]{1,0:T(8,128)(2,1)} custom-call(bf16[96,1792]{1,0:T(8,128)(2,1)} %get-tuple-element.4.share_ref, bf16[3072,2048]{1,0:T(8,128)(2,1)} %bitcast.1), custom_call_target="tpu_custom_call" | custom-call | tf_op jit(solution)/shard_map/finished/pallas_call | solution.py:714
  281.5 4.0 %copy.5 = bf16[768,2048]{1,0:T(8,128)(2,1)} copy(bf16[768,2048]{1,0:T(8,128)(2,1)} %finished.1) | data formatting | bytes 6291456

commit v5 on v4

--- a/solution.py
+++ b/solution.py
@@ -298,7 +298,8 @@
     layout = tuple(sorted(order, key=lambda d: -d[1]))
     shards = math.prod(d[2] for d in layout)
     mine = x_ref.shape[0] // block
-    window = part.shape[0]
+    total = part.shape[0]
+    window = total - mine + 1
     lines = far[2]
     axis = layout[0][0]
     shard = lax.axis_index(axis)
@@ -314,31 +315,31 @@
             t = t - stride if (t // stride) % 2 else t + stride
         return t
 
-    def needed(t, d):
-        wanted = set()
-        for i in range(mine):
-            s, piece = (i + d) // mine % shards, (i + d) % mine
-            if s:
-                wanted.add(((t + s) % shards, piece))
-        return wanted
-
-    slots = [[] for _ in range(window + 1)]
+    arrival = sorted(range(total), key=lambda j: (j // mine > 0, j % mine if j // mine else j, j // mine))
+
+    def needed(t, j):
+        s, piece = j // mine % shards, j % mine
+        return {((t + s) % shards, piece)} if s else set()
+
+    slots = [[] for _ in range(total + 1)]
     done = [0] * shards
-    for d in range(window + 1):
+    early = []
+    for k in range(total + 1):
         begun = {}
         for t in range(shards):
             last = len(events)
-            if d < window:
-                wanted = needed(t, d)
+            if k < total:
+                wanted = needed(t, arrival[k])
                 last = max(
                     [done[t]]
                     + [e + 1 for e, (piece, _, tag) in enumerate(events) if (home(t, tag), piece) in wanted]
                 )
+            if k == total - 1 and last == done[t]:
+                early.append(t)
             for e in range(done[t], last):
                 begun.setdefault(e, []).append(t)
             done[t] = last
-        slots[d] = sorted(begun.items())
-
+        slots[k] = sorted(begun.items())
     copies = {}
 
     def keep(piece, source, condition, tag):
@@ -364,82 +365,100 @@
                 condition = functools.reduce(lambda a, b: a | b, [shard == t for t in who])
                 pl.when(condition)(functools.partial(action, keep))
 
-    def owner_rows(far_place, near_place):
-        start = (far_place * far[1] + near_place * near[1]) * rows
-        return pl.ds(pl.multiple_of(start, 16), rows)
-
-    def near_copy(d, line):
+    def span(j):
+        low, high = max(0, j - window + 1), min(mine - 1, j)
+        return low, high - low + 1
+
+    def near_copy(j):
+        blocks = pl.ds(*span(j))
         return pltpu.make_async_remote_copy(
-            src_ref=part.at[d, owner_rows(line, 1 - place(near)), :],
-            dst_ref=got_near.at[d, line],
-            send_sem=near_send.at[d, line],
-            recv_sem=near_recv.at[d, line],
+            src_ref=part.at[j, blocks, :, 1 - place(near)],
+            dst_ref=got_near.at[j, blocks],
+            send_sem=near_send.at[j],
+            recv_sem=near_recv.at[j],
             device_id=peer(near, 1 - 2 * place(near)),
             device_id_type=pl.DeviceIdType.MESH,
         )
 
-    def far_copy(d, step, arriving):
+    def far_copy(j, step, arriving):
         there, offset = around(far, step)
         slot = there if arriving else place(far)
+        blocks = pl.ds(*span(j))
         return pltpu.make_async_remote_copy(
-            src_ref=half.at[d, there],
-            dst_ref=got_far.at[d, slot],
-            send_sem=far_send.at[d, there],
-            recv_sem=far_recv.at[d, slot],
+            src_ref=half.at[j, there, blocks],
+            dst_ref=got_far.at[j, slot, blocks],
+            send_sem=far_send.at[j, there],
+            recv_sem=far_recv.at[j, slot],
             device_id=peer(far, offset),
             device_id_type=pl.DeviceIdType.MESH,
         )
 
-    def form(d):
-        for i in range(mine):
-            s, piece = (i + d) // mine % shards, (i + d) % mine
-            at = (pl.ds(piece * block, block), slice(None))
-            if s:
-                other = lax.rem(shard + s, shards)
-                at = tuple(lax.rem(lax.div(other, g[1]), g[2]) for g in layout) + at
-                right = held[at]
-            else:
-                right = x_ref[at]
-            left = x_ref[i * block : (i + 1) * block, :]
-            part[d, i * block : (i + 1) * block, :] = nt_dot(left, right).astype(jnp.bfloat16)
-        for line in range(lines):
-            near_copy(d, line).start()
-
-    def halve(d):
-        for line in range(lines):
-            near_copy(d, line).wait_recv()
-            half[d, line] = (
-                part[d, owner_rows(line, place(near)), :].astype(jnp.float32)
-                + got_near[d, line].astype(jnp.float32)
-            ).astype(jnp.bfloat16)
+    def form(k):
+        j = arrival[k]
+        s, piece = j // mine % shards, j % mine
+        at = (pl.ds(piece * block, block), slice(None))
+        if s:
+            other = lax.rem(shard + s, shards)
+            at = tuple(lax.rem(lax.div(other, g[1]), g[2]) for g in layout) + at
+            right = held[at]
+        else:
+            right = x_ref[at]
+        low, size = span(j)
+        product = nt_dot(x_ref[low * block : (low + size) * block, :], right).astype(jnp.bfloat16)
+        for i in range(low, low + size):
+            row = (i - low) * block
+            part[j, i] = product[row : row + block, :].reshape(lines, near[2], rows, block)
+        near_copy(j).start()
+
+    def halve(j):
+        low, size = span(j)
+        near_copy(j).wait_recv()
+        for i in range(low, low + size):
+            for line in range(lines):
+                half[j, line, i] = (
+                    part[j, i, line, place(near)].astype(jnp.float32)
+                    + got_near[j, i, line].astype(jnp.float32)
+                ).astype(jnp.bfloat16)
         for step in range(1, lines):
-            far_copy(d, step, False).start()
-
-    def finish(d):
-        total = half[d, place(far)].astype(jnp.float32)
+            far_copy(j, step, False).start()
+
+    def finish(j):
+        low, size = span(j)
         for step in range(1, lines):
-            there, _ = around(far, step)
-            far_copy(d, step, True).wait_recv()
-            total = total + got_far[d, there].astype(jnp.float32)
-        share_ref[:, d * block : (d + 1) * block] = total.astype(jnp.bfloat16)
-
-    for d in range(window + 2):
-        if d <= window:
-            if d > 0:
-                halve(d - 1)
-            if d > 1:
-                finish(d - 2)
-            advance(d)
+            far_copy(j, step, True).wait_recv()
+        for i in range(low, low + size):
+            value = half[j, place(far), i].astype(jnp.float32)
+            for step in range(1, lines):
+                there, _ = around(far, step)
+                value = value + got_far[j, there, i].astype(jnp.float32)
+            d = j - i
+            share_ref[i * rows : (i + 1) * rows, d * block : (d + 1) * block] = value.astype(jnp.bfloat16)
+
+    def among(who):
+        return functools.reduce(lambda a, b: a | b, [shard == t for t in who])
+
+    split = bool(early) and len(early) < shards
+    for k in range(total):
+        if k > 0:
+            halve(arrival[k - 1])
+        if k > 1:
+            finish(arrival[k - 2])
+        advance(k)
+        if k == total - 1 and split:
+            pl.when(jnp.logical_not(among(early)))(functools.partial(form, k))
         else:
-            finish(d - 2)
-        if d < window:
-            form(d)
-
-    for d in range(window):
-        for line in range(lines):
-            near_copy(d, line).wait_send()
+            form(k)
+        if k == total - 2 and split:
+            pl.when(among(early))(functools.partial(form, total - 1))
+    halve(arrival[total - 1])
+    for j in arrival[-2:]:
+        finish(j)
+    advance(total)
+
+    for j in range(total):
+        near_copy(j).wait_send()
         for step in range(1, lines):
-            far_copy(d, step, False).wait_send()
+            far_copy(j, step, False).wait_send()
     for number, at in copies.items():
         pltpu.make_async_copy(held.at[at], columns_ref.at[at], out_sem.at[number]).wait()
     own.wait()
@@ -448,35 +467,34 @@
 
 def reduced_gram(iterate, digits, block, window, ident):
     layout = tuple(digits["tp"])
-    if len(digits["mats"]) != 2 or any(d[2] != 2 for d in layout):
-        return None
     far, near = digits["mats"]
     mine, width = iterate.shape
-    rows = mine // (far[2] * near[2])
-    if near[2] != 2 or rows % 16 or mine % block:
-        return None
+    rows = block // (far[2] * near[2])
     order = tuple(sorted(layout, key=lambda d: d[3]))
     pieces = [(order, row, block) for row in range(0, mine, block)]
     dims = tuple(d[2] for d in layout)
-    chunks, lines = window // block, far[2]
-    tile = pltpu.VMEM((chunks, lines, rows, block), jnp.bfloat16)
+    own = mine // block
+    total, lines = window // block + own - 1, far[2]
+    near_tile = pltpu.VMEM((total, own, lines, rows, block), jnp.bfloat16)
+    far_tile = pltpu.VMEM((total, lines, own, rows, block), jnp.bfloat16)
     dma = pltpu.SemaphoreType.DMA
     blocks = math.prod(dims) - 1
     columns, share = pl.pallas_call(
         functools.partial(reduce_kernel, block, rows, pieces, far, near),
         out_shape=(
             jax.ShapeDtypeStruct(dims + iterate.shape, jnp.bfloat16),
-            jax.ShapeDtypeStruct((rows, window), jnp.bfloat16),
+            jax.ShapeDtypeStruct((own * rows, window), jnp.bfloat16),
         ),
         in_specs=[pl.BlockSpec(memory_space=pltpu.VMEM)],
         out_specs=(pl.BlockSpec(memory_space=pl.ANY), pl.BlockSpec(memory_space=pltpu.VMEM)),
         scratch_shapes=[
             pltpu.VMEM(dims + iterate.shape, jnp.bfloat16),
-            pltpu.VMEM((chunks, mine, block), jnp.bfloat16),
-            tile, tile, tile,
+            pltpu.VMEM((total, own, lines, near[2], rows, block), jnp.bfloat16),
+            near_tile, far_tile, far_tile,
         ]
         + Gather.semaphores(layout, pieces)
-        + [dma((chunks, lines))] * 4
+        + [dma((total,))] * 2
+        + [dma((total, lines))] * 2
         + [dma((blocks * len(pieces) + 1,))],
         compiler_params=pltpu.CompilerParams(
             collective_id=ident, has_side_effects=True, vmem_limit_bytes=grant
@@ -486,28 +504,42 @@
     return columns.reshape(dims[0] * math.prod(dims[1:]) * mine, width), share
 
 
-def polynomial_rows(gram, own, one, two, left, right, scale, where_ref):
+def polynomial_rows(gram, own, one, two, left, right, raw, sums, scale, where_ref):
     size = gram.shape[0]
-
-    def column_sums(step, total):
-        rows = jnp.abs(gram[pl.ds(pl.multiple_of(step * 16, 16), 16), :].astype(jnp.float32))
-        return total + (rows[0:8] + rows[8:16])
-
-    total = lax.fori_loop(0, size // 16, column_sums, jnp.zeros((8, size), jnp.float32))
-    bound = jnp.max(jnp.sum(total, axis=0, keepdims=True), axis=1, keepdims=True) + epsilon
-    root = lax.rsqrt(jnp.broadcast_to(bound, (1, 128)))
-    inverse = (root * root)[:, :1]
     count = own.shape[0]
     width = math.gcd(size, 1024)
-    if where_ref is None:
-        index = lax.axis_index("tp") * lax.axis_size("mats") + lax.axis_index("mats")
-    else:
-        index = where_ref[0]
-
     def columns(body):
         @pl.loop(0, size // width)
         def _(step):
             body(pl.ds(pl.multiple_of(step * width, width), width))
+
+    if where_ref is None:
+        pass
+    elif count % 16 == 0:
+        own[...] = gram[pl.ds(pl.multiple_of(where_ref[0] * count, 16), count), :]
+    else:
+        row = lax.broadcasted_iota(jnp.int32, (count, size), 0) + where_ref[0] * count
+        column = lax.broadcasted_iota(jnp.int32, (count, size), 1)
+        two[...] = (row == column).astype(jnp.float32).astype(jnp.bfloat16)
+
+        def select(at):
+            own[:, at] = jnp.dot(
+                two[...], gram[:, at], preferred_element_type=jnp.float32
+            ).astype(jnp.bfloat16)
+
+        columns(select)
+
+    tile = math.gcd(size, 512)
+
+    @pl.loop(0, size // tile)
+    def _(step):
+        at = pl.ds(pl.multiple_of(step * tile, tile), tile)
+        raw[:, at] = jnp.dot(own[...], gram[:, at], preferred_element_type=jnp.float32)
+        sums[:, at] = jnp.sum(jnp.abs(gram[:, at].astype(jnp.float32)), axis=0, keepdims=True)
+
+    bound = jnp.max(sums[...], axis=1, keepdims=True) + epsilon
+    root = lax.rsqrt(jnp.broadcast_to(bound, (1, 128)))
+    inverse = (root * root)[:, :1]
 
     def times_gram(source, at):
         return inverse * jnp.dot(source[...], gram[:, at], preferred_element_type=jnp.float32)
@@ -536,28 +568,9 @@
 
         columns(body)
 
-    if count % 16 == 0:
-        own[...] = gram[pl.ds(pl.multiple_of(index * count, 16), count), :]
-    else:
-        row = lax.broadcasted_iota(jnp.int32, (count, size), 0) + index * count
-        column = lax.broadcasted_iota(jnp.int32, (count, size), 1)
-        two[...] = (row == column).astype(jnp.float32).astype(jnp.bfloat16)
-
-        def select(at):
-            own[:, at] = jnp.dot(
-                two[...], gram[:, at], preferred_element_type=jnp.float32
-            ).astype(jnp.bfloat16)
-
-        columns(select)
-
-    def start(at):
-        left[:, at] = (inverse * wide(own, at)).astype(jnp.bfloat16)
-
-    columns(start)
-
     def first(at):
         one[:, at] = (
-            second_coef * wide(left, at) + third_coef * times_gram(left, at)
+            second_coef * (inverse * wide(own, at)) + third_coef * (inverse * (inverse * raw[:, at]))
         ).astype(jnp.bfloat16)
 
     columns(first)
@@ -583,7 +596,7 @@
     return root
 
 
-def poly_kernel(block, scale, where_ref, compact_ref, out_ref, kappa_ref, gram, own, one, two, left, right):
+def poly_kernel(block, scale, where_ref, compact_ref, out_ref, kappa_ref, gram, own, one, two, left, right, raw, sums):
     size = gram.shape[0]
     blocks = size // block
     window = compact_ref.shape[1] // block
@@ -595,14 +608,14 @@
             if d > 0 and 2 * d != blocks:
                 gram[j * block : (j + 1) * block, i * block : (i + 1) * block] = tile.T
 
-    root = polynomial_rows(gram, own, one, two, left, right, scale, where_ref)
+    root = polynomial_rows(gram, own, one, two, left, right, raw, sums, scale, where_ref)
     kappa_ref[...] = (scale * first_coef * first_coef) * root
     out_ref[...] = left[...]
 
 
 def finish_kernel(
     block, scale, layout, pieces, near_pieces, share_ref, columns_ref, out_ref, held, gram, own, one, two, left,
-    right, rows, columns, result, send_sem, recv_sem, rows_send, rows_recv, in_sem, out_sem,
+    right, raw, sums, rows, columns, result, send_sem, recv_sem, rows_send, rows_recv, in_sem, out_sem,
 ):
     barrier_all(layout)
     tp = tuple(d for d in layout if d[0] == "tp")
@@ -624,20 +637,25 @@
     blocks = size // block
     shards = math.prod(d[2] for d in tp)
     mine = size // shards
+    own_blocks = mine // block
+    seg = count // own_blocks
     for t in range(shards):
         at = tuple((t // d[1]) % d[2] for d in tp)
         for d in range(window // block):
-            strip = held[at + (slice(None), slice(None), slice(None), pl.ds(d * block, block))]
-            strip = strip.reshape(mine, block)
-            for k in range(mine // block):
-                i = t * (mine // block) + k
+            for k in range(own_blocks):
+                i = t * own_blocks + k
                 j = (i + d) % blocks
-                tile = strip[k * block : (k + 1) * block, :]
+                tile = held[at + (slice(None), slice(None), pl.ds(k * seg, seg), pl.ds(d * block, block))]
+                tile = tile.reshape(block, block)
                 gram[i * block : (i + 1) * block, j * block : (j + 1) * block] = tile
                 if d > 0 and 2 * d != blocks:
                     gram[j * block : (j + 1) * block, i * block : (i + 1) * block] = tile.T
 
-    root = polynomial_rows(gram, own, one, two, left, right, scale, None)
+    first = lax.axis_index("tp") * mine + lax.axis_index("mats") * seg
+    for k in range(own_blocks):
+        at = pl.ds(pl.multiple_of(first + k * block, 16), seg)
+        own[k * seg : (k + 1) * seg, :] = gram[at, :]
+    root = polynomial_rows(gram, own, one, two, left, right, raw, sums, scale, None)
     kappa = ((scale * first_coef * first_coef) * root)[:, :1]
 
     spread = Gather((far, near), near_pieces, rows, left, rows_send, rows_recv)
@@ -653,18 +671,21 @@
 
     def multiply(line):
         matrix = rows[line].reshape(pair, size)
-        at = pl.ds(pl.multiple_of(line * pair, 16), pair)
-        mirror = pl.ds(pl.multiple_of(shard_row + line * pair, 16), pair)
 
         @pl.loop(0, columns.shape[1] // width)
         def _(step):
             across = pl.ds(pl.multiple_of(step * width, width), width)
             product = jnp.dot(matrix, columns[:, across], preferred_element_type=jnp.float32)
-            result[at, across] = (
-                product + kappa * columns[mirror, across].astype(jnp.float32)
-            ).astype(jnp.bfloat16)
-
-        pltpu.make_async_copy(result.at[at], out_ref.at[at], out_sem.at[line]).start()
+            for n in range(near[2]):
+                for k in range(own_blocks):
+                    start = shard_row + k * block + (line * near[2] + n) * seg
+                    mirror = columns[pl.ds(pl.multiple_of(start, 16), seg), across]
+                    row = n * count + k * seg
+                    result[k, line, n * seg : (n + 1) * seg, across] = (
+                        product[row : row + seg, :] + kappa * mirror.astype(jnp.float32)
+                    ).astype(jnp.bfloat16)
+
+        pltpu.make_async_copy(result.at[:, line], out_ref.at[:, line], out_sem.at[line]).start()
 
     groups = [(None, place(far), None)]
     groups += [((far, hop, travel), q, there) for hop, travel, q, there in relatives(far)]
@@ -685,8 +706,7 @@
                 if not wanted:
                     when(there, functools.partial(multiply, q))
     for line in range(far[2]):
-        at = pl.ds(line * pair, pair)
-        pltpu.make_async_copy(result.at[at], out_ref.at[at], out_sem.at[line]).wait()
+        pltpu.make_async_copy(result.at[:, line], out_ref.at[:, line], out_sem.at[line]).wait()
     gather.drain()
     spread.drain()
 
@@ -694,13 +714,9 @@
 def finished(share, columns, digits, block, scale, ident):
     layout, _ = orders_of(digits)
     count, window = share.shape
-    if len(digits["mats"]) != 2 or len(digits["tp"]) != 2 or digits["mats"][1][2] != 2 or count % 16:
-        return None
     far, near = digits["mats"]
     side = [d for d in digits["tp"] if not d[3]]
     close = tuple(d for d in digits["tp"] if d[3])
-    if len(side) != 1 or any(d[2] != 2 for d in digits["tp"]):
-        return None
     orders = [(far, near, side[0]) + close, (far, side[0], near) + close]
     pieces = pieces_of(count, orders, 2)
     most = (count * 5 // 6 + 15) // 16 * 16
@@ -711,9 +727,10 @@
     dims = tuple(d[2] for d in layout)
     mine = count * far[2] * near[2]
     thin = pltpu.VMEM((count, size), jnp.bfloat16)
+    shape = (mine // block, far[2], block // far[2], width)
     return pl.pallas_call(
         functools.partial(finish_kernel, block, scale, layout, pieces, near_pieces),
-        out_shape=jax.ShapeDtypeStruct((mine, width), jnp.bfloat16),
+        out_shape=jax.ShapeDtypeStruct(shape, jnp.bfloat16),
         in_specs=[pl.BlockSpec(memory_space=pltpu.VMEM), pl.BlockSpec(memory_space=pl.ANY)],
         out_specs=pl.BlockSpec(memory_space=pl.ANY),
         scratch_shapes=[
@@ -722,9 +739,11 @@
         ]
         + [thin] * 5
         + [
+            pltpu.VMEM((count, size), jnp.float32),
+            pltpu.VMEM((1, size), jnp.float32),
             pltpu.VMEM((far[2], near[2], count, size), jnp.bfloat16),
             pltpu.VMEM((size, width), jnp.bfloat16),
-            pltpu.VMEM((mine, width), jnp.bfloat16),
+            pltpu.VMEM(shape, jnp.bfloat16),
         ]
         + Gather.semaphores(layout, pieces)
         + Gather.semaphores((far, near), near_pieces)
@@ -733,7 +752,16 @@
             collective_id=ident, has_side_effects=True, vmem_limit_bytes=63 * 1024 * 1024
         ),
         name="finished",
-    )(share, columns)
+    )(share, columns).reshape(mine, width)
+
+
+def paired(digits, block):
+    tp, mats = digits["tp"], digits["mats"]
+    if len(tp) != 2 or len(mats) != 2 or mats[1][2] != 2 or any(d[2] != 2 for d in tp):
+        return False
+    if sum(not d[3] for d in tp) != 1:
+        return False
+    return block % (16 * mats[0][2] * mats[1][2]) == 0
 
 
 def orders_of(digits):
@@ -758,24 +786,19 @@
     whole = pl.BlockSpec(memory_space=pltpu.VMEM)
     params = pltpu.CompilerParams(vmem_limit_bytes=grant)
     tp = lax.axis_index("tp")
-    fused = reduced_gram(iterate, digits, block, window, 1)
-    if fused is not None:
-        columns, share = fused
-    else:
-        columns = gather(iterate, "tp", tuple(digits["tp"]), [lines["tp"]], 6, 1, "gather_x")
-        part = pl.pallas_call(
-            functools.partial(gram_kernel, block),
-            out_shape=jax.ShapeDtypeStruct((mine, window), jnp.bfloat16),
-            in_specs=[smem, whole],
-            out_specs=whole,
-            compiler_params=params,
-            name="gram",
-        )(tp.reshape(1), columns)
-        share = lax.psum_scatter(part, "mats", scatter_dimension=0, tiled=True)
-    if fused is not None:
-        update = finished(share, columns, digits, block, scale, 2)
-        if update is not None:
-            return (update, new_momentum)
+    if paired(digits, block):
+        columns, share = reduced_gram(iterate, digits, block, window, 1)
+        return (finished(share, columns, digits, block, scale, 2), new_momentum)
+    columns = gather(iterate, "tp", tuple(digits["tp"]), [lines["tp"]], 6, 1, "gather_x")
+    part = pl.pallas_call(
+        functools.partial(gram_kernel, block),
+        out_shape=jax.ShapeDtypeStruct((mine, window), jnp.bfloat16),
+        in_specs=[smem, whole],
+        out_specs=whole,
+        compiler_params=params,
+        name="gram",
+    )(tp.reshape(1), columns)
+    share = lax.psum_scatter(part, "mats", scatter_dimension=0, tiled=True)
     compact = gather(share, ("tp", "mats"), layout, orders, 2, 2, "gather_gram")
     count = share.shape[0]
     place = tp * lax.axis_size("mats") + lax.axis_index("mats")
@@ -788,7 +811,9 @@
         ),
         in_specs=[smem, whole],
         out_specs=(whole, whole),
-        scratch_shapes=[pltpu.VMEM((size, size), jnp.bfloat16)] + [thin] * 5,
+        scratch_shapes=[pltpu.VMEM((size, size), jnp.bfloat16)]
+        + [thin] * 5
+        + [pltpu.VMEM((count, size), jnp.float32), pltpu.VMEM((1, size), jnp.float32)],
         compiler_params=params,
         cost_estimate=pl.CostEstimate(
             flops=22 * count * size * size, bytes_accessed=size * window * 2, transcendentals=0

time: 286 us -> 282 us (0.986)
  Pallas kernels: 272 us -> 268 us
    pallas_call x1, Pallas kernels: 107 us -> 95 us  [reduced_gram(): pl.pallas_call(functools.partial(reduce_kernel, block, rows, pieces, far,...]
    pallas_call x1, Pallas kernels: 165 us -> 173 us  [finished(): pl.pallas_call(functools.partial(finish_kernel, block, scale, layout, pie...]
where the time goes in v5:
time: 282 us
  Pallas kernels  268 us (95%)
  other arithmetic  9.26 us (3%)
  local copies, waits for them, and re-layouts  3.97 us (1%)
    pallas_call x1, Pallas kernels, finished(): pl.pallas_call(functools.partial(finish_kernel, block, scale, layout, pie...  173 us
    pallas_call x1, Pallas kernels, reduced_gram(): pl.pallas_call(functools.partial(reduce_kernel, block, rows, pieces, far,...  95 us
    convert_element_type x1, other arithmetic, per_device(): (grad.astype(jnp.float32) + momentum_beta * new_momentum).astype(jnp.bflo...  9.26 us

profile of v5, /device:TPU:0, one launch (start us, length us, event | category | flops | bytes accessed | tf_op | source)
XLA Modules:
  0.0 282.1 jit_solution(5117543973422569410)
XLA Ops:
  0.6 9.3 %fusion = (bf16[768,2048]{1,0:T(8,128)(2,1)}, f32[768,2048]{1,0:T(8,128)}) fusion(bf16[768,2048]{1,0:T(8,128)(2,1)} %param.2, f32[768,2048]{1,0:T(8,128)} %param.3), kind=kLoop, calls=%fused_computation.2 | loop fusion | flops 9437184 | bytes 18874368 | tf_op jit(solution)/shard_map/convert_element_type | solution.py:778
  9.9 95.0 %reduced_gram.1 = (bf16[2,2,768,2048]{3,2,1,0:T(8,128)(2,1)}, bf16[96,1792]{1,0:T(8,128)(2,1)}) custom-call(bf16[768,2048]{1,0:T(8,128)(2,1)} %get-tuple-element.6.x_ref), custom_call_target="tpu_custom_call" | custom-call | tf_op jit(solution)/shard_map/reduced_gram/pallas_call | solution.py:482
  104.9 173.1 %finished.1 = bf16[3,4,64,2048]{3,2,1,0:T(8,128)(2,1)} custom-call(bf16[96,1792]{1,0:T(8,128)(2,1)} %get-tuple-element.4.share_ref, bf16[3072,2048]{1,0:T(8,128)(2,1)} %bitcast.2), custom_call_target="tpu_custom_call" | custom-call | tf_op jit(solution)/shard_map/finished/pallas_call | solution.py:731
  278.1 4.0 %copy.5 = bf16[768,2048]{1,0:T(8,128)(2,1)} copy(bf16[768,2048]{1,0:T(8,128)(2,1)} %bitcast.3) | data formatting | bytes 6291456

commit v6 on v5

--- a/solution.py
+++ b/solution.py
@@ -306,7 +306,6 @@
     barrier_lines(layout + (far, near))
     gather = Gather(layout, pieces, held, x_ref, send_sem, recv_sem)
     queue = gather.queue()
-    starts = [entry for entry in queue if not entry[2]]
     events = [entry for entry in queue if entry[2]]
 
     def home(t, tag):
@@ -315,11 +314,23 @@
             t = t - stride if (t // stride) % 2 else t + stride
         return t
 
-    arrival = sorted(range(total), key=lambda j: (j // mine > 0, j % mine if j // mine else j, j // mine))
+    arrival = list(range(total))
 
     def needed(t, j):
         s, piece = j // mine % shards, j % mine
         return {((t + s) % shards, piece)} if s else set()
+
+    side, close = order
+
+    def rank(t, e):
+        piece, _, tag = events[e]
+        if len(tag) == 2:
+            kind = 1 if (t // close[1]) % 2 else 2
+        else:
+            kind = 0 if tag[0][0] == close else 2 if (t // close[1]) % 2 else 1
+        return kind, piece
+
+    turns = [sorted(range(len(events)), key=functools.partial(rank, t)) for t in range(shards)]
 
     slots = [[] for _ in range(total + 1)]
     done = [0] * shards
@@ -332,11 +343,15 @@
                 wanted = needed(t, arrival[k])
                 last = max(
                     [done[t]]
-                    + [e + 1 for e, (piece, _, tag) in enumerate(events) if (home(t, tag), piece) in wanted]
+                    + [
+                        turn + 1
+                        for turn, e in enumerate(turns[t])
+                        if (home(t, events[e][2]), events[e][0]) in wanted
+                    ]
                 )
             if k == total - 1 and last == done[t]:
                 early.append(t)
-            for e in range(done[t], last):
+            for e in turns[t][done[t] : last]:
                 begun.setdefault(e, []).append(t)
             done[t] = last
         slots[k] = sorted(begun.items())
@@ -349,21 +364,35 @@
         copies[number] = at
         pltpu.make_async_copy(held.at[at], columns_ref.at[at], out_sem.at[number]).start()
 
-    for _, action, _ in starts:
-        action(None)
+    here = {d: place(d) for d in layout}
+    ahead = here[close] == 0
+    for piece in range(len(pieces)):
+        gather.send(piece, here, ahead, side, None, (), own=True)
+        gather.sent[(piece, (), side, 0)] = (here, None, True)
+        gather.send(piece, here, None, close, None, (), own=True)
     own = pltpu.make_async_copy(
         x_ref, columns_ref.at[tuple(place(d) for d in layout)], out_sem.at[len(events)]
     )
     own.start()
 
+    def handle(e):
+        piece, action, tag = events[e]
+        action(keep)
+        last = len(pieces) - 1
+        if len(tag) == 2 and piece >= last - 1:
+            freed = range(1) if piece < last else range(1 if last else 0, last + 1)
+            offset, _ = moves(side)[0]
+            for p in freed:
+                copy = gather.copy(p, here, side, offset, 0, True)
+                pl.when(jnp.logical_not(ahead))(copy.start)
+
     def advance(d):
         for e, who in slots[d]:
-            _, action, _ = events[e]
             if len(who) == shards:
-                action(keep)
+                handle(e)
             else:
                 condition = functools.reduce(lambda a, b: a | b, [shard == t for t in who])
-                pl.when(condition)(functools.partial(action, keep))
+                pl.when(condition)(functools.partial(handle, e))
 
     def span(j):
         low, high = max(0, j - window + 1), min(mine - 1, j)
@@ -759,7 +788,7 @@
     tp, mats = digits["tp"], digits["mats"]
     if len(tp) != 2 or len(mats) != 2 or mats[1][2] != 2 or any(d[2] != 2 for d in tp):
         return False
-    if sum(not d[3] for d in tp) != 1:
+    if tp[0][3] or not tp[1][3]:
         return False
     return block % (16 * mats[0][2] * mats[1][2]) == 0
 

time: 282 us -> 266 us (0.943)
  Pallas kernels: 268 us -> 251 us
    pallas_call x1, Pallas kernels: 173 us -> 158 us  [finished(): pl.pallas_call(functools.partial(finish_kernel, block, scale, layout, pie...]
where the time goes in v6:
time: 266 us; the launch traced here: 265 us
  Pallas kernels  251 us (94%)
  other arithmetic  9.26 us (3%)
  local copies, waits for them, and re-layouts  3.97 us (1%)
    pallas_call x1, Pallas kernels, finished(): pl.pallas_call(functools.partial(finish_kernel, block, scale, layout, pie...  158 us
    pallas_call x1, Pallas kernels, reduced_gram(): pl.pallas_call(functools.partial(reduce_kernel, block, rows, pieces, far,...  93.3 us
    convert_element_type x1, other arithmetic, per_device(): (grad.astype(jnp.float32) + momentum_beta * new_momentum).astype(jnp.bflo...  9.26 us

profile of v6, /device:TPU:0, one launch (start us, length us, event | category | flops | bytes accessed | tf_op | source)
XLA Modules:
  0.0 265.4 jit_solution(13754424592819684023)
XLA Ops:
  0.6 9.3 %fusion = (bf16[768,2048]{1,0:T(8,128)(2,1)}, f32[768,2048]{1,0:T(8,128)}) fusion(bf16[768,2048]{1,0:T(8,128)(2,1)} %param.2, f32[768,2048]{1,0:T(8,128)} %param.3), kind=kLoop, calls=%fused_computation.2 | loop fusion | flops 9437184 | bytes 18874368 | tf_op jit(solution)/shard_map/convert_element_type | solution.py:807
  9.9 93.3 %reduced_gram.1 = (bf16[2,2,768,2048]{3,2,1,0:T(8,128)(2,1)}, bf16[96,1792]{1,0:T(8,128)(2,1)}) custom-call(bf16[768,2048]{1,0:T(8,128)(2,1)} %get-tuple-element.6.x_ref), custom_call_target="tpu_custom_call" | custom-call | tf_op jit(solution)/shard_map/reduced_gram/pallas_call | solution.py:511
  103.2 158.2 %finished.1 = bf16[3,4,64,2048]{3,2,1,0:T(8,128)(2,1)} custom-call(bf16[96,1792]{1,0:T(8,128)(2,1)} %get-tuple-element.4.share_ref, bf16[3072,2048]{1,0:T(8,128)(2,1)} %bitcast.2), custom_call_target="tpu_custom_call" | custom-call | tf_op jit(solution)/shard_map/finished/pallas_call | solution.py:760
  261.4 4.0 %copy.5 = bf16[768,2048]{1,0:T(8,128)(2,1)} copy(bf16[768,2048]{1,0:T(8,128)(2,1)} %bitcast.3) | data formatting | bytes 6291456
